TPU v7x, 8 devices: a whole 2x2x1 slice. The times are simulated.
8 devices in a mesh: dp: 1 (over z), tp: 8 (over y, x, core).
Axes of the slice: x: 2, y: 2, z: 1, core: 2. Of those that a mesh axis runs over, the one named last changes fastest.
Arguments:
- residual: float32 [256, 4096], P('dp')
- norm_w: bfloat16 [2, 4096], replicated
- w_in: bfloat16 [2, 4096, 2, 8192], P(None, None, None, 'tp')
- conv_w: bfloat16 [2, 4, 8192], P(None, None, 'tp')
- conv_b: bfloat16 [2, 8192], P(None, 'tp')
- w_x: bfloat16 [2, 8192, 288], P(None, 'tp')
- w_dt: bfloat16 [2, 256, 8192], P(None, None, 'tp')
- b_dt: float32 [2, 8192], P(None, 'tp')
- a_log: float32 [2, 16, 8192], P(None, None, 'tp')
- d_skip: float32 [2, 8192], P(None, 'tp')
- w_out: bfloat16 [2, 8192, 4096], P(None, 'tp')
- conv_state: bfloat16 [2, 256, 3, 8192], P(None, 'dp', None, 'tp')
- ssm_state: float32 [2, 256, 16, 8192], P(None, 'dp', None, 'tp')
Outputs:
- output 1: float32 [256, 4096], P('dp')
- output 2: bfloat16 [2, 256, 3, 8192], P(None, 'dp', None, 'tp')
- output 3: float32 [2, 256, 16, 8192], P(None, 'dp', None, 'tp')
All inputs are finite; a program needn't handle non-finite values.
Results may differ from a plain program's by a relative error of at most 0.0192232.
Values are sent between devices in bfloat16 or wider.
A program may use at most 1 GiB of HBM per device.

v0:
```python
import jax
import jax.numpy as jnp
from jax import lax
from jax.sharding import PartitionSpec as P


def rms_norm(vector, epsilon):
    return vector * lax.rsqrt(jnp.mean(vector * vector, axis=-1, keepdims=True) + epsilon)


def solution(mesh):
    def device_step(residual, norm_w, w_in, conv_w, conv_b, w_x, w_dt, b_dt, a_log, d_skip, w_out, conv_state, ssm_state):
        rank_dim = w_dt.shape[1]
        state_dim = a_log.shape[1]
        conv_list = []
        ssm_list = []
        for layer_idx in range(norm_w.shape[0]):
            hidden = (rms_norm(residual, 1e-5) * norm_w[layer_idx].astype(jnp.float32)).astype(jnp.bfloat16)
            xz_val = jnp.einsum('bd,dwe->bwe', hidden, w_in[layer_idx], preferred_element_type=jnp.float32).astype(jnp.bfloat16)
            window = jnp.concatenate([conv_state[layer_idx], xz_val[:, 0:1, :]], axis=1)
            conv_pre = jnp.sum(window.astype(jnp.float32) * conv_w[layer_idx].astype(jnp.float32), axis=1) + conv_b[layer_idx].astype(jnp.float32)
            x_conv = jax.nn.silu(conv_pre).astype(jnp.bfloat16)
            proj_part = jnp.dot(x_conv, w_x[layer_idx], preferred_element_type=jnp.float32).astype(jnp.bfloat16)
            proj_sum = lax.psum(proj_part, 'tp').astype(jnp.float32)
            dt_low = rms_norm(proj_sum[:, :rank_dim], 1e-6).astype(jnp.bfloat16)
            b_vec = rms_norm(proj_sum[:, rank_dim:rank_dim + state_dim], 1e-6)
            c_vec = rms_norm(proj_sum[:, rank_dim + state_dim:], 1e-6)
            dt_val = jax.nn.softplus(jnp.dot(dt_low, w_dt[layer_idx], preferred_element_type=jnp.float32) + b_dt[layer_idx])
            x_float = x_conv.astype(jnp.float32)
            decay_fac = jnp.exp(dt_val[:, None, :] * -jnp.exp(a_log[layer_idx]))
            new_ssm = decay_fac * ssm_state[layer_idx] + (dt_val * x_float)[:, None, :] * b_vec[:, :, None]
            y_val = jnp.sum(new_ssm * c_vec[:, :, None], axis=1) + d_skip[layer_idx] * x_float
            gated_y = (y_val * jax.nn.silu(xz_val[:, 1, :].astype(jnp.float32))).astype(jnp.bfloat16)
            out_part = jnp.dot(gated_y, w_out[layer_idx], preferred_element_type=jnp.float32).astype(jnp.bfloat16)
            residual = residual + lax.psum(out_part, 'tp').astype(jnp.float32)
            conv_list.append(window[:, 1:, :])
            ssm_list.append(new_ssm)
        return residual, jnp.stack(conv_list), jnp.stack(ssm_list)

    cache_spec = P(None, 'dp', None, 'tp')
    in_specs = (P('dp', None), P(None, None), P(None, None, None, 'tp'), P(None, None, 'tp'), P(None, 'tp'), P(None, 'tp', None), P(None, None, 'tp'), P(None, 'tp'), P(None, None, 'tp'), P(None, 'tp'), P(None, 'tp', None), cache_spec, cache_spec)
    out_specs = (P('dp', None), cache_spec, cache_spec)
    return jax.shard_map(device_step, mesh=mesh, in_specs=in_specs, out_specs=out_specs, check_vma=False)
```

profile of v0, /device:TPU:0, one launch (start us, length us, event | category | flops | bytes accessed | tf_op | source)
XLA Modules:
  0.0 338.2 jit_solution(11131427526303613223)
XLA Ops:
  7.3 2.7 multiply_reduce_fusion.3
  10.0 0.6 slice_convert_fusion.2
  10.6 0.6 slice_convert_fusion.1
  11.2 0.4 slice_bitcast_fusion
  11.6 26.2 %fusion.68 = (bf16[1,4096,2,1024]{3,2,1,0:T(2,128)(2,1)}, bf16[1,4096,2,1024]{3,2,1,0:T(2,128)(2,1)}) fusion(bf16[2,4096,2,1024]{3,2,1,0:T(2,128)(2,1)} %param.15), kind=kLoop, calls=%fused_computation.128 | loop fusion | bytes 67108864 | tf_op jit(solution)/shard_map/slice | solution.py:19
  37.8 11.3 %fusion.32 = bf16[256,2,1024]{2,0,1:T(8,128)(2,1)S(1)} fusion(bf16[1,4096,2,1024]{3,2,1,0:T(2,128)(2,1)} %get-tuple-element.9, f32[256,4096]{1,0:T(8,128)S(1)} %copy-done, f32[4096]{0:T(1024)S(1)} %bitcast.131, f32[256]{0:T(256)S(1)} %add_rsqrt_fusion.7), kind=kOutput, calls=%fused_computation.52 | convolution fusion | flops 4298637312 | bytes 22037504 | tf_op jit(solution)/shard_map/bd,dwe->bwe/dot_general | solution.py:19
  49.2 0.8 copy-done.6
  50.0 0.4 multiply_reduce_fusion.2
  50.4 1.0 copy-done.16
  51.4 1.2 convolution_convert_fusion.1
  52.6 0.2 all-reduce.7.cloned.1.call-start
  52.8 0.6 fusion.70
  53.5 0.6 negate_bitcast_fusion
  54.1 0.6 fusion.69
  54.7 43.3 %all-reduce.5.cloned.1.call-done = bf16[256,288]{0,1:T(8,128)(2,1)} async-done(((bf16[256,288]{0,1:T(8,128)(2,1)}), bf16[256,288]{0,1:T(8,128)(2,1)}) %all-reduce.5.cloned.1.call-update) | async-done | bytes 147472 | tf_op jit(solution)/shard_map/psum | solution.py:24
  98.0 0.9 convert_element_type.133
  98.9 0.1 multiply_reduce_fusion.5
  99.0 0.6 add_rsqrt_fusion.6
  99.6 0.8 copy.17
  100.4 0.7 copy.18
  101.1 2.4 convert_multiply_fusion.3
  103.6 10.2 %fusion.7 = f32[256,1024]{1,0:T(8,128)S(1)} fusion(f32[2,256,16,1024]{3,2,1,0:T(8,128)} %param.25, f32[256,16]{1,0:T(8,128)S(1)} %copy-done.20, f32[256,16]{1,0:T(8,128)S(1)} %copy-done.12, f32[256,1024]{1,0:T(8,128)S(1)} %get-tuple-element.29, f32[16,1024]{1,0:T(8,128)S(1)} %copy-done.18, f32[256,1024]{1,0:T(8,128)S(1)} %get-tuple-element.30), kind=kLoop, calls=%fused_computation.12 | loop fusion | flops 24903680 | bytes 20021248 | tf_op jit(solution)/shard_map/reduce_sum | solution.py:32
  113.9 7.4 %fusion.14 = bf16[256,4096]{1,0:T(8,128)(2,1)} fusion(bf16[2,1024,4096]{2,1,0:T(8,128)(2,1)} %param.23, f32[256,1024]{1,0:T(8,128)S(1)} %fusion.7, f32[256,1024]{1,0:T(8,128)S(1)} %copy-done.17, bf16[256,2,1024]{2,0,1:T(8,128)(2,1)S(1)} %copy-done.24, f32[1024]{0:T(1024)S(1)} %bitcast.139, f32[1024]{0:T(1024)S(1)} %bitcast.140), kind=kOutput, calls=%fused_computation.21 | convolution fusion | flops 2152726528 | bytes 13115392 | tf_op jit(solution)/shard_map/dot_general | solution.py:34
  121.3 0.3 all-reduce.9.cloned.1.call-start
  121.6 2.3 fusion.31
  123.9 46.9 %all-reduce.7.cloned.1.call-done = bf16[256,4096]{1,0:T(8,128)(2,1)} async-done(((bf16[256,4096]{1,0:T(8,128)(2,1)}), bf16[256,4096]{1,0:T(8,128)(2,1)}) %all-reduce.7.cloned.1.call-update) | async-done | bytes 2097168 | tf_op jit(solution)/shard_map/psum | solution.py:35
  170.9 3.6 %multiply_reduce_fusion.1 = f32[256]{0:T(256)S(1)} fusion(f32[256,4096]{1,0:T(8,128)} %param.13, bf16[256,4096]{1,0:T(8,128)(2,1)} %all-reduce.7.cloned.1.call-done), kind=kLoop, calls=%fused_computation.26 | loop fusion | flops 4194048 | bytes 6292480 | tf_op jit(solution)/shard_map/reduce_sum | solution.py:8
  174.5 0.4 copy-done.1
  174.9 0.7 copy-done.2
  175.6 11.4 %fusion.35 = bf16[256,2,1024]{2,0,1:T(8,128)(2,1)S(1)} fusion(bf16[1,4096,2,1024]{3,2,1,0:T(2,128)(2,1)} %get-tuple-element.10, f32[4096]{0:T(1024)S(1)} %bitcast.130, f32[256]{0:T(256)S(1)} %add_rsqrt_fusion.3, f32[256,4096]{1,0:T(8,128)S(1)} %copy-done.1, bf16[256,4096]{1,0:T(8,128)(2,1)S(1)} %copy-done.2), kind=kOutput, calls=%fused_computation.53 | convolution fusion | flops 4300734464 | bytes 24134656 | tf_op jit(solution)/shard_map/bd,dwe->bwe/dot_general | solution.py:19
  187.1 1.3 fusion.29
  188.4 0.4 multiply_reduce_fusion
  188.9 0.9 copy-done.14
  189.8 1.2 convolution_convert_fusion
  191.0 0.3 all-reduce.11.cloned.1.call-start
  191.4 1.9 pad_maximum_fusion.1
  193.3 39.5 %all-reduce.9.cloned.1.call-done = bf16[256,288]{0,1:T(8,128)(2,1)} async-done(((bf16[256,288]{0,1:T(8,128)(2,1)}), bf16[256,288]{0,1:T(8,128)(2,1)}) %all-reduce.9.cloned.1.call-update) | async-done | bytes 147472 | tf_op jit(solution)/shard_map/psum | solution.py:24
  232.8 0.9 convert_element_type.148
  233.8 0.1 multiply_reduce_fusion.4
  233.9 0.1 copy.20
  234.0 0.1 copy.21
  234.1 2.5 convert_multiply_fusion.2
  236.7 22.5 %multiply_add_fusion.1 = (f32[1,256,16,1024]{3,2,1,0:T(8,128)}, f32[1,256,16,1024]{3,2,1,0:T(8,128)}) fusion(f32[2,256,16,1024]{3,2,1,0:T(8,128)} %param.25, f32[256,16]{1,0:T(8,128)S(1)} %copy-done.13, f32[256,1024]{1,0:T(8,128)S(1)} %copy-done.8, f32[16,1024]{1,0:T(8,128)S(1)} %copy-done.19, f32[256,1024]{1,0:T(8,128)S(1)} %copy-done.10, ...), kind=kLoop, calls=%fused_computation.14 | loop fusion | flops 33554432 | bytes 71467008 | tf_op jit(solution)/shard_map/add | solution.py:31
  259.2 9.6 %fusion.4 = f32[256,1024]{1,0:T(8,128)S(1)} fusion(f32[2,256,16,1024]{3,2,1,0:T(8,128)} %param.25, f32[256,16]{1,0:T(8,128)S(1)} %copy.21, f32[256,16]{1,0:T(8,128)S(1)} %copy.20, f32[256,1024]{1,0:T(8,128)S(1)} %get-tuple-element.31, f32[16,1024]{1,0:T(8,128)S(1)} %get-tuple-element.17, f32[256,1024]{1,0:T(8,128)S(1)} %get-tuple-element.32), kind=kLoop, calls=%fused_computation.8 | loop fusion | flops 24903680 | bytes 20021248 | tf_op jit(solution)/shard_map/reduce_sum | solution.py:32
  268.9 7.4 %fusion.17 = bf16[256,4096]{1,0:T(8,128)(2,1)} fusion(bf16[2,1024,4096]{2,1,0:T(8,128)(2,1)} %param.23, f32[256,1024]{1,0:T(8,128)S(1)} %fusion.4, f32[256,1024]{1,0:T(8,128)S(1)} %copy-done.15, bf16[256,2,1024]{2,0,1:T(8,128)(2,1)S(1)} %copy-done.22, f32[1024]{0:T(1024)S(1)} %bitcast.134, f32[1024]{0:T(1024)S(1)} %bitcast.135), kind=kOutput, calls=%fused_computation.22 | convolution fusion | flops 2152726528 | bytes 13115392 | tf_op jit(solution)/shard_map/dot_general | solution.py:34
  276.3 24.0 %pad_maximum_fusion = f32[2,256,16,1024]{3,2,1,0:T(8,128)} fusion(f32[1,256,16,1024]{3,2,1,0:T(8,128)} %get-tuple-element.8, f32[1,256,16,1024]{3,2,1,0:T(8,128)} %get-tuple-element.7), kind=kLoop, calls=%fused_computation | loop fusion | flops 8388608 | bytes 67108864 | tf_op jit(solution)/shard_map/stack | solution.py:38
  300.3 25.6 %all-reduce.11.cloned.1.call-done = bf16[256,4096]{1,0:T(8,128)(2,1)} async-done(((bf16[256,4096]{1,0:T(8,128)(2,1)}), bf16[256,4096]{1,0:T(8,128)(2,1)}) %all-reduce.11.cloned.1.call-update) | async-done | bytes 2097168 | tf_op jit(solution)/shard_map/psum | solution.py:35
  325.9 5.8 %convert_add_fusion = f32[256,4096]{1,0:T(8,128)} fusion(bf16[256,4096]{1,0:T(8,128)(2,1)} %all-reduce.11.cloned.1.call-done, f32[256,4096]{1,0:T(8,128)} %param.13, bf16[256,4096]{1,0:T(8,128)(2,1)S(1)} %copy-done.3), kind=kLoop, calls=%fused_computation.23 | loop fusion | flops 4194304 | bytes 12582912 | tf_op jit(solution)/shard_map/add | solution.py:35
  (93 shorter events, 0.4 us)
Async XLA Ops:
  7.2 2.8 copy-start.28
  7.2 3.4 %copy-start.26 = (bf16[2,4096]{1,0:T(2,128)(2,1)S(1)}, bf16[2,4096]{1,0:T(2,128)(2,1)}, u32[]{:S(2)}) copy-start(bf16[2,4096]{1,0:T(2,128)(2,1)} %param.14) | copy-start | bytes 49156
  7.2 4.0 %copy-start.27 = (bf16[2,4,1024]{2,1,0:T(4,128)(2,1)S(1)}, bf16[2,4,1024]{2,1,0:T(4,128)(2,1)}, u32[]{:S(2)}) copy-start(bf16[2,4,1024]{2,1,0:T(4,128)(2,1)} %param.16) | copy-start | bytes 49156
  7.2 90.8 %all-reduce.5.cloned.1.call-start = ((), (), s32[]{:S(2)}) async-start(), calls=%async_computation | async-start | bytes 294912 | tf_op jit(solution)/shard_map/psum | solution.py:24
  7.2 4.0 %copy-start.11 = (bf16[2,256,3,1024]{3,1,2,0:T(8,128)(2,1)S(1)}, bf16[2,256,3,1024]{3,1,2,0:T(8,128)(2,1)}, u32[]{:S(2)}) copy-start(bf16[2,256,3,1024]{3,1,2,0:T(8,128)(2,1)} %param.24) | copy-start | bytes 9437188
  10.6 39.9 %copy-start.35 = (f32[1,1024]{1,0:T(1,128)}, f32[1,1024]{1,0:T(1,128)S(1)}, u32[]{:S(2)}) copy-start(f32[1,1024]{1,0:T(1,128)S(1)} %get-tuple-element.28) | copy-start | bytes 12292
  11.6 26.2 %copy-start = (f32[256,4096]{1,0:T(8,128)S(1)}, f32[256,4096]{1,0:T(8,128)}, u32[]{:S(2)}) copy-start(f32[256,4096]{1,0:T(8,128)} %param.13) | copy-start | bytes 12582916
  49.1 1.3 copy-start.23
  49.1 2.3 copy-start.38
  49.2 0.8 copy-start.6
  50.0 2.9 copy-start.30
  50.0 3.5 %copy-start.25 = (f32[2,16,1024]{2,1,0:T(8,128)S(1)}, f32[2,16,1024]{2,1,0:T(8,128)}, u32[]{:S(2)}) copy-start(f32[2,16,1024]{2,1,0:T(8,128)} %param.21) | copy-start | bytes 393220
  50.0 4.1 %copy-start.31 = (f32[2,1024]{1,0:T(2,128)S(1)}, f32[2,1024]{1,0:T(2,128)}, u32[]{:S(2)}) copy-start(f32[2,1024]{1,0:T(2,128)} %param.22) | copy-start | bytes 24580
  50.4 1.0 copy-start.16
  52.6 118.3 %all-reduce.7.cloned.1.call-start = ((), (), s32[]{:S(2)}) async-start(), calls=%async_computation.1 | async-start | bytes 4194304 | tf_op jit(solution)/shard_map/psum | solution.py:35
  101.1 2.5 copy-start.12
  101.1 2.5 copy-start.18
  101.1 2.5 copy-start.20
  103.5 10.3 %copy-start.7 = (f32[256,1024]{1,0:T(8,128)}, f32[256,1024]{1,0:T(8,128)S(1)}, u32[]{:S(2)}) copy-start(f32[256,1024]{1,0:T(8,128)S(1)} %get-tuple-element.29) | copy-start | bytes 3145732
  103.5 10.3 %copy-start.9 = (f32[256,1024]{1,0:T(8,128)}, f32[256,1024]{1,0:T(8,128)S(1)}, u32[]{:S(2)}) copy-start(f32[256,1024]{1,0:T(8,128)S(1)} %get-tuple-element.30) | copy-start | bytes 3145732
  103.6 10.3 %copy-start.17 = (f32[256,1024]{1,0:T(8,128)S(1)}, f32[256,1024]{1,0:T(8,128)}, u32[]{:S(2)}) copy-start(f32[256,1024]{1,0:T(8,128)} %copy-done.16) | copy-start | bytes 3145732
  103.6 10.3 %copy-start.24 = (bf16[256,2,1024]{2,0,1:T(8,128)(2,1)S(1)}, bf16[256,2,1024]{2,0,1:T(8,128)(2,1)}, u32[]{:S(2)}) copy-start(bf16[256,2,1024]{2,0,1:T(8,128)(2,1)} %copy-done.23) | copy-start | bytes 3145732
  103.6 10.3 %copy-start.36 = (f32[1,1024]{1,0:T(1,128)S(1)}, f32[1,1024]{1,0:T(1,128)}, u32[]{:S(2)}) copy-start(f32[1,1024]{1,0:T(1,128)} %copy-done.35) | copy-start | bytes 12292
  103.6 10.3 %copy-start.37 = (f32[1,1024]{1,0:T(1,128)S(1)}, f32[1,1024]{1,0:T(1,128)}, u32[]{:S(2)}) copy-start(f32[1,1024]{1,0:T(1,128)} %get-tuple-element.24) | copy-start | bytes 12292
  121.3 53.2 %copy-start.29 = (f32[1,4096]{1,0:T(1,128)S(1)}, f32[1,4096]{1,0:T(1,128)}, u32[]{:S(2)}) copy-start(f32[1,4096]{1,0:T(1,128)} %get-tuple-element.22) | copy-start | bytes 49156
  121.3 111.5 %all-reduce.9.cloned.1.call-start = ((), (), s32[]{:S(2)}) async-start(), calls=%async_computation.2 | async-start | bytes 294912 | tf_op jit(solution)/shard_map/psum | solution.py:24
  170.9 4.1 %copy-start.1 = (f32[256,4096]{1,0:T(8,128)S(1)}, f32[256,4096]{1,0:T(8,128)}, u32[]{:S(2)}) copy-start(f32[256,4096]{1,0:T(8,128)} %param.13) | copy-start | bytes 12582916
  170.9 4.7 %copy-start.2 = (bf16[256,4096]{1,0:T(8,128)(2,1)S(1)}, bf16[256,4096]{1,0:T(8,128)(2,1)}, u32[]{:S(2)}) copy-start(bf16[256,4096]{1,0:T(8,128)(2,1)} %all-reduce.7.cloned.1.call-done) | copy-start | bytes 6291460
  187.0 1.8 copy-start.21
  187.1 2.8 copy-start.32
  187.1 2.8 copy-start.39
  188.4 3.0 copy-start.4
  188.9 1.0 copy-start.14
  188.9 2.5 copy-start.5
  191.0 43.1 %copy-start.34 = (f32[1,1024]{1,0:T(1,128)S(1)}, f32[1,1024]{1,0:T(1,128)}, u32[]{:S(2)}) copy-start(f32[1,1024]{1,0:T(1,128)} %get-tuple-element.25) | copy-start | bytes 12292
  191.0 134.8 %all-reduce.11.cloned.1.call-start = ((), (), s32[]{:S(2)}) async-start(), calls=%async_computation.3 | async-start | bytes 4194304 | tf_op jit(solution)/shard_map/psum | solution.py:35
  234.1 2.6 copy-start.8
  234.1 2.6 copy-start.10
  234.1 2.6 copy-start.13
  234.1 2.6 copy-start.19
  259.2 9.6 %copy-start.15 = (f32[256,1024]{1,0:T(8,128)S(1)}, f32[256,1024]{1,0:T(8,128)}, u32[]{:S(2)}) copy-start(f32[256,1024]{1,0:T(8,128)} %copy-done.14) | copy-start | bytes 3145732
  259.2 9.6 %copy-start.22 = (bf16[256,2,1024]{2,0,1:T(8,128)(2,1)S(1)}, bf16[256,2,1024]{2,0,1:T(8,128)(2,1)}, u32[]{:S(2)}) copy-start(bf16[256,2,1024]{2,0,1:T(8,128)(2,1)} %copy-done.21) | copy-start | bytes 3145732
  259.2 9.6 %copy-start.33 = (f32[1,1024]{1,0:T(1,128)S(1)}, f32[1,1024]{1,0:T(1,128)}, u32[]{:S(2)}) copy-start(f32[1,1024]{1,0:T(1,128)} %get-tuple-element.23) | copy-start | bytes 12292
  276.3 49.6 %copy-start.3 = (bf16[256,4096]{1,0:T(8,128)(2,1)S(1)}, bf16[256,4096]{1,0:T(8,128)(2,1)}, u32[]{:S(2)}) copy-start(bf16[256,4096]{1,0:T(8,128)(2,1)} %all-reduce.7.cloned.1.call-done) | copy-start | bytes 6291460
Sparse Core Ops, SparseCore 0:
  52.7 45.1 all-reduce.4
  121.5 49.3 all-reduce.6
  191.2 41.6 all-reduce.8
  276.4 49.3 all-reduce.10
where the time goes:
time: 339 us; the launch traced here: 338 us
  waiting for transfers between devices  155 us (46%)
  other arithmetic  89.3 us (26%)
  matrix products  44.8 us (13%)
  local copies, waits for them, and re-layouts  33.5 us (10%)
  between operations  14.3 us (4%)
    psum x2, waiting for transfers between devices, device_step(): proj_sum = lax.psum(proj_part, 'tp').astype(jnp.float32)  82.8 us
    psum x2, waiting for transfers between devices, device_step(): residual = residual + lax.psum(out_part, 'tp').astype(jnp.float32)  72.5 us
    another operation x4, other arithmetic, device_step(): return (residual, jnp.stack(conv_list), jnp.stack(ssm_list))  29.5 us
    slice x1, local copies, waits for them, and re-layouts, device_step(): w_in[layer_idx]  26.2 us
    dot_general x2, matrix products, device_step(): jnp.einsum('bd,dwe->bwe', hidden, w_in[layer_idx], preferred_element_type...  22.7 us
    add x1, other arithmetic, device_step(): decay_fac * ssm_state[layer_idx]  22.5 us
    reduce_sum x2, other arithmetic, device_step(): jnp.sum(new_ssm * c_vec[:, :, None], axis=1) + d_skip[layer_idx] * x_float  19.8 us
    dot_general x2, matrix products, device_step(): jnp.dot(gated_y, w_out[layer_idx], preferred_element_type=jnp.float32)  14.8 us
  transfers between devices with their start and end apart: 4, of which 4 were waited for; matrix products, arithmetic and copies ran while one was open for 9% of the time, Pallas kernels for 0%

commit v1 on v0

v1 whole, which is shorter than its diff:
```python
import functools

import jax
import jax.numpy as jnp
from jax import lax
from jax.experimental import pallas as pl
from jax.experimental.pallas import tpu as pltpu
from jax.sharding import PartitionSpec as P

F32 = jnp.float32
BF16 = jnp.bfloat16
MESH = pl.DeviceIdType.MESH
VMEM = pl.BlockSpec(memory_space=pltpu.VMEM)
ANY = pl.BlockSpec(memory_space=pl.ANY)
DMA = pltpu.SemaphoreType.DMA

TOK = 256
DIM = 4096
CH = 1024
PW = 288
NST = 16
RANK = 256
NCH = 4
CW = DIM // NCH
NW = 8
KD = 256


def rows(start, size):
    return pl.ds(pl.multiple_of(start, size), size)


def place():
    me = lax.axis_index("tp")
    core = lax.rem(me, 2)
    xb = lax.rem(lax.div(me, 2), 2)
    yb = lax.div(me, 4)
    partner = me + 1 - 2 * core
    xn = me + 2 - 4 * xb
    yn = me + 4 - 8 * yb
    first = xn * (1 - core) + yn * core
    second = yn * (1 - core) + xn * core
    fb = xb * (1 - core) + yb * core
    sb = yb * (1 - core) + xb * core
    return core, fb, sb, partner, first, second


def enter(peers):
    barrier = pltpu.get_barrier_semaphore()
    for peer in peers:
        pl.semaphore_signal(barrier, inc=1, device_id={"tp": peer}, device_id_type=MESH)
    return lambda: pl.semaphore_wait(barrier, len(peers))


def remote(src, dst, sems, idx, to):
    return pltpu.make_async_remote_copy(
        src_ref=src, dst_ref=dst, send_sem=sems.at[0, idx], recv_sem=sems.at[1, idx],
        device_id={"tp": to}, device_id_type=MESH)


def spread(parity):
    src = lax.broadcasted_iota(jnp.int32, (128, 256), 0)
    dst = lax.broadcasted_iota(jnp.int32, (128, 256), 1)
    return jnp.where(dst == 2 * src + parity, 1.0, 0.0).astype(BF16)


def proj_steps(lo, hi, parity, acc, h, w):
    sel = spread(parity)

    def step(i, carry):
        cols = rows(i * KD, KD)
        hc = h[:, cols]
        lhs = jnp.concatenate(
            [jnp.dot(hc[:, j * 128:(j + 1) * 128], sel, preferred_element_type=F32).astype(BF16)
             for j in range(KD // 128)], axis=1)
        wc = w[cols].reshape(2 * KD, CH)
        acc[...] += jnp.dot(lhs, wc, preferred_element_type=F32)
        return carry

    lax.fori_loop(lo, hi, step, 0)


def w_in_copies(layer, w_in, w, sem):
    size = DIM // NW
    return [pltpu.make_async_copy(w_in.at[layer, pl.ds(i * size, size)], w.at[pl.ds(i * size, size)], sem.at[i])
            for i in range(NW)]


def conv_stage(acc, cs, conv_w, conv_b, x, xc):
    def block(i, carry):
        r = rows(i * 32, 32)
        xv = acc[r, :].astype(BF16)
        x[r, :] = xv
        pre = cs[0, r, :].astype(F32) * conv_w[0:1, :]
        pre += cs[1, r, :].astype(F32) * conv_w[1:2, :]
        pre += cs[2, r, :].astype(F32) * conv_w[2:3, :]
        pre += xv.astype(F32) * conv_w[3:4, :]
        pre += conv_b[...]
        xc[r, :] = (pre * jax.nn.sigmoid(pre)).astype(BF16)
        return carry

    lax.fori_loop(0, TOK // 32, block, 0)


def p_stage(where, z_part, xc, wx, p, ptx, prx, psem):
    core, _, _, partner, first, second = where

    def half(index):
        return lax.dot_general(wx[...], xc[rows(index * 128, 128), :], (((1,), (1,)), ((), ())),
                               preferred_element_type=F32)

    ptx[0] = half(1 - core).astype(BF16)
    hop = remote(ptx.at[0], prx.at[0], psem, 0, partner)
    hop.start()
    p[core] = half(core)
    z_part(0)
    hop.wait()
    for k, to in ((1, first), (2, second), (3, partner)):
        p[core] += prx[k - 1].astype(F32)
        ptx[k] = p[core].astype(BF16)
        hop = remote(ptx.at[k], prx.at[k], psem, k, to)
        hop.start()
        z_part(k)
        hop.wait()
    p[1 - core] = prx[3].astype(F32)


def in_tail(where, acc, h, w, cs, conv_w, conv_b, wx, x, xc, z, p, ptx, prx, psem):
    conv_stage(acc, cs, conv_w, conv_b, x, xc)
    acc[...] = jnp.zeros_like(acc)
    n = DIM // KD
    cuts = (0, n // 8, n // 2, n - n // 8, n)

    def z_part(k):
        proj_steps(cuts[k], cuts[k + 1], 1, acc, h, w)

    p_stage(where, z_part, xc, wx, p, ptx, prx, psem)

    def block(i, carry):
        r = rows(i * 32, 32)
        z[r, :] = acc[r, :].astype(BF16)
        return carry

    lax.fori_loop(0, TOK // 32, block, 0)


def first_kernel(resid, norm_w, w_in, conv_w, conv_b, wx_hbm, cs_hbm, x, xc, z, p,
                 h, w, acc, rbuf, wx, cs, ptx, prx, wsem, lsem, psem):
    where = place()
    core, fb, sb, partner, first, second = where
    await_peers = enter((partner, first, second))
    nr = 8
    rcopies = [pltpu.make_async_copy(resid.at[pl.ds(i * 32, 32)], rbuf.at[pl.ds(i * 32, 32)], lsem.at[2 + i])
               for i in range(nr)]
    for c in rcopies:
        c.start()
    wcopies = w_in_copies(0, w_in, w, wsem)
    for c in wcopies:
        c.start()
    small = [pltpu.make_async_copy(wx_hbm.at[0], wx, lsem.at[0]), pltpu.make_async_copy(cs_hbm.at[0], cs, lsem.at[1])]
    for c in small:
        c.start()
    acc[...] = jnp.zeros_like(acc)

    for c in rcopies:
        c.wait()

    def norm_block(i, carry):
        r = rows(i * 16, 16)
        v = rbuf[r, :]
        scale = lax.rsqrt(jnp.mean(v * v, axis=-1, keepdims=True) + 1e-5)
        h[r, :] = (v * scale * norm_w[...]).astype(BF16)
        return carry

    lax.fori_loop(0, TOK // 16, norm_block, 0)
    per = DIM // NW // KD
    for i in range(NW):
        wcopies[i].wait()
        proj_steps(i * per, (i + 1) * per, 0, acc, h, w)
    for c in small:
        c.wait()
    await_peers()
    in_tail(where, acc, h, w, cs, conv_w, conv_b, wx, x, xc, z, p, ptx, prx, psem)


def reduce_scatter(where, await_peers, yg, wout, wcopies, own, tx0, rx0, tx1, rx1, tx2, rx2, rsem):
    core, fb, sb, partner, first, second = where
    col = [pl.ds(c * CW, CW) for c in range(NCH)]
    hop0 = [remote(tx0.at[:, col[c]], rx0.at[:, col[c]], rsem, c, partner) for c in range(NCH)]
    hop1 = [remote(tx1.at[:, col[c]], rx1.at[:, col[c]], rsem, NCH + c, first) for c in range(NCH)]
    hop2 = [remote(tx2.at[:, col[c]], rx2.at[:, col[c]], rsem, 2 * NCH + c, second) for c in range(NCH)]

    def product(c):
        wcopies[c].wait()
        wc = wout[:, col[c]]
        tx0[:, col[c]] = jnp.dot(yg[rows((1 - core) * 128, 128), :], wc, preferred_element_type=F32).astype(BF16)
        if c == 0:
            await_peers()
        hop0[c].start()
        own[:, col[c]] = jnp.dot(yg[rows(core * 128, 128), :], wc, preferred_element_type=F32)

    def stage1(c):
        hop0[c].wait()
        give, keep = rows((1 - fb) * 64, 64), rows(fb * 64, 64)
        tx1[:, col[c]] = (own[give, col[c]] + rx0[give, col[c]].astype(F32)).astype(BF16)
        hop1[c].start()
        own[keep, col[c]] += rx0[keep, col[c]].astype(F32)

    def stage2(c):
        hop1[c].wait()
        give, keep = (1 - sb) * 32, sb * 32
        tx2[:, col[c]] = (own[rows(fb * 64 + give, 32), col[c]] + rx1[rows(give, 32), col[c]].astype(F32)).astype(BF16)
        hop2[c].start()
        own[rows(fb * 64 + keep, 32), col[c]] += rx1[rows(keep, 32), col[c]].astype(F32)

    product(0)
    product(1)
    stage1(0)
    product(2)
    stage1(1)
    product(3)
    stage1(2)
    stage1(3)
    for c in range(NCH):
        stage2(c)
    mine = rows(fb * 64 + sb * 32, 32)
    for c in range(NCH):
        hop2[c].wait()
        own[mine, col[c]] += rx2[:, col[c]].astype(F32)
    return mine


def all_gather(where, h, gsem, consume):
    core, fb, sb, partner, first, second = where
    col = [pl.ds(c * CW, CW) for c in range(NCH)]
    base = core * 128

    def hops(k, start, size, to):
        part = [h.at[rows(start, size), col[c]] for c in range(NCH)]
        return [remote(part[c], part[c], gsem, k * NCH + c, to) for c in range(NCH)]

    hop0 = hops(0, base + fb * 64 + sb * 32, 32, second)
    hop1 = hops(1, base + fb * 64, 64, first)
    hop2 = hops(2, base, 128, partner)
    for c in range(NCH):
        hop0[c].start()
    for c in range(NCH):
        hop0[c].wait()
        hop1[c].start()
    for c in range(NCH):
        hop1[c].wait()
        hop2[c].start()
    for c in range(NCH):
        hop2[c].wait()
        consume(c)


def w_out_copies(layer, w_out, wout, sem):
    return [pltpu.make_async_copy(w_out.at[layer, :, pl.ds(c * CW, CW)], wout.at[:, pl.ds(c * CW, CW)], sem.at[c])
            for c in range(NCH)]


def middle_kernel(yg, w_out, resid, norm_w, w_in, conv_w, conv_b, wx_hbm, cs_hbm, x, xc, z, p, oshard,
                  wout, own, tx0, rx0, tx1, rx1, tx2, rx2, rmine,
                  h, w, acc, wx, cs, ptx, prx, osem, wsem, lsem, rsem, gsem, psem):
    where = place()
    core, fb, sb, partner, first, second = where
    await_peers = enter((partner, first, second))
    ocopies = w_out_copies(0, w_out, wout, osem)
    for c in ocopies:
        c.start()
    row0 = core * 128 + fb * 64 + sb * 32
    small = [pltpu.make_async_copy(wx_hbm.at[1], wx, lsem.at[0]), pltpu.make_async_copy(cs_hbm.at[1], cs, lsem.at[1]),
             pltpu.make_async_copy(resid.at[rows(row0, 32)], rmine, lsem.at[2])]
    for c in small:
        c.start()
    wcopies = w_in_copies(1, w_in, w, wsem)
    for c in wcopies:
        c.start()
    acc[...] = jnp.zeros_like(acc)
    mine = reduce_scatter(where, await_peers, yg, wout, ocopies, own, tx0, rx0, tx1, rx1, tx2, rx2, rsem)
    small[2].wait()
    for b in range(2):
        sub = pl.ds(pl.multiple_of(fb * 64 + sb * 32 + b * 16, 16), 16)
        o = own[sub, :]
        oshard[b * 16:(b + 1) * 16, :] = o
        v = o + rmine[b * 16:(b + 1) * 16, :]
        scale = lax.rsqrt(jnp.mean(v * v, axis=-1, keepdims=True) + 1e-5)
        h[pl.ds(pl.multiple_of(row0 + b * 16, 16), 16), :] = (v * scale * norm_w[...]).astype(BF16)
    for c in wcopies:
        c.wait()
    per = CW // KD
    all_gather(where, h, gsem, lambda c: proj_steps(c * per, (c + 1) * per, 0, acc, h, w))
    small[0].wait()
    small[1].wait()
    in_tail(where, acc, h, w, cs, conv_w, conv_b, wx, x, xc, z, p, ptx, prx, psem)


def last_kernel(yg, w_out, oshard, out, wout, own, tx0, rx0, tx1, rx1, tx2, rx2, total, osem, rsem, gsem, csem):
    where = place()
    core, fb, sb, partner, first, second = where
    await_peers = enter((partner, first, second))
    ocopies = w_out_copies(1, w_out, wout, osem)
    for c in ocopies:
        c.start()
    reduce_scatter(where, await_peers, yg, wout, ocopies, own, tx0, rx0, tx1, rx1, tx2, rx2, rsem)
    row0 = core * 128 + fb * 64 + sb * 32
    for b in range(2):
        sub = pl.ds(pl.multiple_of(fb * 64 + sb * 32 + b * 16, 16), 16)
        total[pl.ds(pl.multiple_of(row0 + b * 16, 16), 16), :] = (own[sub, :] + oshard[b * 16:(b + 1) * 16, :]).astype(BF16)
    outs = [pltpu.make_async_copy(total.at[:, pl.ds(c * CW, CW)], out.at[:, pl.ds(c * CW, CW)], csem.at[c])
            for c in range(NCH)]
    all_gather(where, total, gsem, lambda c: outs[c].start())
    for c in outs:
        c.wait()


NB = 16
TB = TOK // NB


def ssm_kernel(layer, p, x, xc, z, w_dt, b_dt, a_log, d_skip, cs_hbm, st_hbm, *refs):
    if layer:
        refs = refs[2:]
    yg, conv_out, st_out, st, dt_raw, dts, us, ys, a, bc, cs, isem, osem, csem = refs
    ins = [pltpu.make_async_copy(st_hbm.at[layer, pl.ds(i * TB, TB)], st.at[pl.ds(i * TB, TB)], isem.at[i])
           for i in range(NB)]
    for c in ins:
        c.start()
    cin = pltpu.make_async_copy(cs_hbm.at[layer, pl.ds(1, 2)], cs, csem.at[0])
    cin.start()
    a[...] = -jnp.exp(a_log[...])
    for hf in range(2):
        low = p[hf, 0:RANK, :]
        low = low * lax.rsqrt(jnp.mean(low * low, axis=0, keepdims=True) + 1e-6)
        dt_raw[hf * 128:(hf + 1) * 128, :] = lax.dot_general(
            low.astype(BF16), w_dt[...], (((0,), (0,)), ((), ())), preferred_element_type=F32)
        for k in range(2):
            v = p[hf, RANK + k * NST:RANK + (k + 1) * NST, :]
            bc[hf, k * NST:(k + 1) * NST, :] = v * lax.rsqrt(jnp.mean(v * v, axis=0, keepdims=True) + 1e-6)
    cin.wait()
    couts = [pltpu.make_async_copy(cs, conv_out.at[layer, pl.ds(0, 2)], csem.at[1]),
             pltpu.make_async_copy(x, conv_out.at[layer, 2], csem.at[2])]
    for c in couts:
        c.start()

    def block(i, carry):
        r = rows(i * TB, TB)
        pltpu.make_async_copy(st_hbm.at[layer, r], st.at[r], isem.at[i]).wait()
        dt = jax.nn.softplus(dt_raw[r, :] + b_dt[...])
        xf = xc[r, :].astype(F32)
        dts[...] = dt
        us[...] = dt * xf
        hf = lax.div(i, NB // 2)
        shift = lax.rem(128 - lax.rem(i, NB // 2) * TB, 128)
        bct = pltpu.roll(bc[hf], shift, 1)
        for j in range(TB):
            bx = bct[0:NST, j:j + 1]
            cx = bct[NST:2 * NST, j:j + 1]
            s = jnp.exp(dts[j:j + 1, :] * a[...]) * st[i * TB + j] + us[j:j + 1, :] * bx
            st[i * TB + j] = s
            ys[j:j + 1, :] = jnp.sum(s * cx, axis=0, keepdims=True)
        pltpu.make_async_copy(st.at[r], st_out.at[layer, r], osem.at[i]).start()
        zf = z[r, :].astype(F32)
        y = ys[...] + d_skip[...] * xf
        yg[r, :] = (y * (zf * jax.nn.sigmoid(zf))).astype(BF16)
        return carry

    lax.fori_loop(0, NB, block, 0)
    for c in couts:
        c.wait()
    for i in range(NB):
        pltpu.make_async_copy(st.at[pl.ds(i * TB, TB)], st_out.at[layer, pl.ds(i * TB, TB)], osem.at[i]).wait()


def sds(shape, dtype):
    return jax.ShapeDtypeStruct(shape, dtype)


IN_OUTS = (sds((TOK, CH), BF16), sds((TOK, CH), BF16), sds((TOK, CH), BF16), sds((2, PW, 128), F32))
P_SCRATCH = [pltpu.VMEM((4, PW, 128), BF16), pltpu.VMEM((4, PW, 128), BF16)]
RS_SCRATCH = [pltpu.VMEM((CH, DIM), BF16), pltpu.VMEM((128, DIM), F32)] + [
    pltpu.VMEM((n, DIM), BF16) for n in (128, 128, 64, 64, 32, 32)]


def params(collective_id=None, mib=60):
    if collective_id is None:
        return pltpu.CompilerParams(vmem_limit_bytes=mib << 20)
    return pltpu.CompilerParams(vmem_limit_bytes=mib << 20, collective_id=collective_id, has_side_effects=True)


def solution(mesh):
    def first_call(residual, norm_w, w_in, conv_w, conv_b, wx, cs):
        return pl.pallas_call(
            first_kernel, out_shape=IN_OUTS, in_specs=[ANY, VMEM, ANY, VMEM, VMEM, ANY, ANY], out_specs=(VMEM,) * 4,
            scratch_shapes=[pltpu.VMEM((TOK, DIM), BF16), pltpu.VMEM((DIM, 2, CH), BF16), pltpu.VMEM((TOK, CH), F32),
                            pltpu.VMEM((TOK, DIM), F32), pltpu.VMEM((PW, CH), BF16), pltpu.VMEM((3, TOK, CH), BF16),
                            *P_SCRATCH, DMA((NW,)), DMA((10,)), DMA((2, 4))],
            compiler_params=params(0), name="first",
        )(residual, norm_w, w_in, conv_w, conv_b, wx, cs)

    def middle_call(yg, w_out, residual, norm_w, w_in, conv_w, conv_b, wx, cs):
        return pl.pallas_call(
            middle_kernel, out_shape=(*IN_OUTS, sds((32, DIM), F32)),
            in_specs=[VMEM, ANY, ANY, VMEM, ANY, VMEM, VMEM, ANY, ANY], out_specs=(VMEM,) * 5,
            scratch_shapes=[*RS_SCRATCH, pltpu.VMEM((32, DIM), F32),
                            pltpu.VMEM((TOK, DIM), BF16), pltpu.VMEM((DIM, 2, CH), BF16), pltpu.VMEM((TOK, CH), F32),
                            pltpu.VMEM((PW, CH), BF16), pltpu.VMEM((3, TOK, CH), BF16), *P_SCRATCH,
                            DMA((NCH,)), DMA((NW,)), DMA((3,)), DMA((2, 3 * NCH)), DMA((2, 3 * NCH)), DMA((2, 4))],
            compiler_params=params(1), name="middle",
        )(yg, w_out, residual, norm_w, w_in, conv_w, conv_b, wx, cs)

    def last_call(yg, w_out, oshard):
        return pl.pallas_call(
            last_kernel, out_shape=sds((TOK, DIM), BF16), in_specs=[VMEM, ANY, VMEM], out_specs=ANY,
            scratch_shapes=[*RS_SCRATCH, pltpu.VMEM((TOK, DIM), BF16),
                            DMA((NCH,)), DMA((2, 3 * NCH)), DMA((2, 3 * NCH)), DMA((NCH,))],
            compiler_params=params(2), name="last",
        )(yg, w_out, oshard)

    def ssm_call(layer, p, x, xc, z, w_dt, b_dt, a_log, d_skip, cs, st, held=()):
        return pl.pallas_call(
            functools.partial(ssm_kernel, layer),
            out_shape=(sds((TOK, CH), BF16), sds(cs.shape, BF16), sds(st.shape, F32)),
            in_specs=[VMEM] * 8 + [ANY, ANY] + [ANY] * len(held), out_specs=(VMEM, ANY, ANY),
            input_output_aliases={10: 1, 11: 2} if held else {},
            scratch_shapes=[pltpu.VMEM((TOK, NST, CH), F32), pltpu.VMEM((TOK, CH), F32), pltpu.VMEM((TB, CH), F32),
                            pltpu.VMEM((TB, CH), F32), pltpu.VMEM((TB, CH), F32), pltpu.VMEM((NST, CH), F32),
                            pltpu.VMEM((2, 2 * NST, 128), F32), pltpu.VMEM((2, TOK, CH), BF16),
                            DMA((NB,)), DMA((NB,)), DMA((3,))],
            compiler_params=params(), name=f"ssm{layer}",
        )(p, x, xc, z, w_dt, b_dt, a_log, d_skip, cs, st, *held)

    def device_step(residual, norm_w, w_in, conv_w, conv_b, w_x, w_dt, b_dt, a_log, d_skip, w_out, conv_state, ssm_state):
        cs = jnp.swapaxes(conv_state, 1, 2)
        wx = jnp.swapaxes(w_x, 1, 2)
        norm_w, conv_w, conv_b = norm_w.astype(F32), conv_w.astype(F32), conv_b.astype(F32)

        def conv_args(layer):
            return norm_w[layer:layer + 1], w_in, conv_w[layer], conv_b[layer:layer + 1], wx, cs

        def ssm_args(layer):
            return w_dt[layer], b_dt[layer:layer + 1], a_log[layer], d_skip[layer:layer + 1], cs, ssm_state

        x, xc, z, p = first_call(residual, *conv_args(0))
        yg, conv_out, ssm_out = ssm_call(0, p, x, xc, z, *ssm_args(0))
        x, xc, z, p, oshard = middle_call(yg, w_out, residual, *conv_args(1))
        yg, conv_out, ssm_out = ssm_call(1, p, x, xc, z, *ssm_args(1), (conv_out, ssm_out))
        total = last_call(yg, w_out, oshard)
        return residual + total.astype(F32), jnp.swapaxes(conv_out, 1, 2), ssm_out

    cache_spec = P(None, 'dp', None, 'tp')
    in_specs = (P('dp', None), P(None, None), P(None, None, None, 'tp'), P(None, None, 'tp'), P(None, 'tp'), P(None, 'tp', None), P(None, None, 'tp'), P(None, 'tp'), P(None, None, 'tp'), P(None, 'tp'), P(None, 'tp', None), cache_spec, cache_spec)
    out_specs = (P('dp', None), cache_spec, cache_spec)
    return jax.shard_map(device_step, mesh=mesh, in_specs=in_specs, out_specs=out_specs, check_vma=False)
```

time: 339 us -> 175 us (0.52)
  Pallas kernels: 0 us -> 159 us
  waiting for transfers between devices: 155 us -> 0 us
  other arithmetic: 89.3 us -> 6.32 us
  matrix products: 44.8 us -> 0 us
  local copies, waits for them, and re-layouts: 33.5 us -> 8.56 us
  between operations: 14.3 us -> 0.67 us
    pallas_call x0 -> x5, Pallas kernels: none -> 159 us  [the longest x1 55.6 us: middle_call(): pl.pallas_call(middle_kernel, out_shape=(*IN_OUTS, sds((32, DIM), F32)),...]
    psum x4 -> x0, waiting for transfers between devices: 155 us -> none  [the longest x2 82.8 us: device_step(): proj_sum = lax.psum(proj_part, 'tp').astype(jnp.float32)]
    dot_general x8 -> x0, matrix products: 44.8 us -> none  [the longest x2 22.7 us: device_step(): jnp.einsum('bd,dwe->bwe', hidden, w_in[layer_idx], preferred_element_type...]
    another operation x4 -> x0, other arithmetic: 29.5 us -> none  [device_step(): return (residual, jnp.stack(conv_list), jnp.stack(ssm_list))]
    reduce_sum x10 -> x0, other arithmetic: 27.2 us -> none  [the longest x2 19.8 us: device_step(): jnp.sum(new_ssm * c_vec[:, :, None], axis=1) + d_skip[layer_idx] * x_float]
    slice x5 -> x3, local copies, waits for them, and re-layouts: 27.5 us -> 4.18 us  [the longest x1 1.43 us: conv_args(): norm_w[layer:layer + 1]]
    add x3 -> x1, other arithmetic: 28.9 us -> 5.6 us  [device_step(): return (residual + total.astype(F32), jnp.swapaxes(conv_out, 1, 2), ssm_out)]
    squeeze x1 -> x3, local copies, waits for them, and re-layouts: 0.36 us -> 4.38 us  [the longest x1 2.24 us: ssm_args(): w_dt[layer]]
  transfers between devices with their start and end apart: 4 -> 0, of which waited for: 4 -> 0; matrix products, arithmetic and copies ran while one was open for 9% -> 0% of each run, Pallas kernels for 0% -> 0%
where the time goes in v1:
time: 175 us
  Pallas kernels  159 us (91%)
  local copies, waits for them, and re-layouts  8.56 us (5%)
  other arithmetic  6.32 us (4%)
    pallas_call x1, Pallas kernels, middle_call(): pl.pallas_call(middle_kernel, out_shape=(*IN_OUTS, sds((32, DIM), F32)),...  55.6 us
    pallas_call x2, Pallas kernels, ssm_call(): pl.pallas_call(functools.partial(ssm_kernel, layer), out_shape=(sds((TOK,...  38.5 us
    pallas_call x1, Pallas kernels, last_call(): pl.pallas_call(last_kernel, out_shape=sds((TOK, DIM), BF16), in_specs=[VM...  32.8 us
    pallas_call x1, Pallas kernels, first_call(): pl.pallas_call(first_kernel, out_shape=IN_OUTS, in_specs=[ANY, VMEM, ANY,...  32.4 us
    add x1, other arithmetic, device_step(): return (residual + total.astype(F32), jnp.swapaxes(conv_out, 1, 2), ssm_out)  5.6 us

profile of v1, /device:TPU:0, one launch (start us, length us, event | category | flops | bytes accessed | tf_op | source)
XLA Modules:
  0.0 174.9 jit_solution(3054556251169047432)
XLA Ops:
  0.6 1.4 fusion.3
  2.0 1.4 fusion.1
  3.4 0.7 convert_element_type.13
  4.1 0.6 slice_bitcast_fusion.4
  4.7 1.4 fusion
  6.1 1.5 slice_bitcast_fusion.2
  7.7 2.2 %slice_bitcast_fusion = (bf16[256,1024]{1,0:T(8,128)(2,1)}, bf16[256,1024]{1,0:T(8,128)(2,1)}) fusion(bf16[2,256,1024]{2,1,0:T(8,128)(2,1)} %param.19), kind=kLoop, calls=%fused_computation.1 | loop fusion | bytes 2097152 | tf_op jit(solution)/shard_map/squeeze | solution.py:443
  9.9 32.4 %first.1 = (bf16[256,1024]{1,0:T(8,128)(2,1)}, bf16[256,1024]{1,0:T(8,128)(2,1)}, bf16[256,1024]{1,0:T(8,128)(2,1)}, f32[2,288,128]{2,1,0:T(8,128)}) custom-call(f32[256,4096]{1,0:T(8,128)} %resid.3, f32[1,4096]{1,0:T(1,128)} %get-tuple-element.40.norm_w, bf16[2,4096,2,1024]{3,2,1,0:T(2,128)(2,1)} %w_in.3, f32[4,1024]{1,0:T(4,128)} %get-tuple-element.38.conv_w, ...), custom_call_target="tpu_custom_call" | custom-call | tf_op jit(solution)/shard_map/first/pallas_call | solution.py:394
  42.4 19.2 %ssm0.1 = (bf16[256,1024]{1,0:T(8,128)(2,1)}, bf16[2,3,256,1024]{3,2,1,0:T(8,128)(2,1)}, f32[2,256,16,1024]{3,2,1,0:T(8,128)}) custom-call(f32[2,288,128]{2,1,0:T(8,128)} %get-tuple-element.18.p, bf16[256,1024]{1,0:T(8,128)(2,1)} %get-tuple-element.19.x, bf16[256,1024]{1,0:T(8,128)(2,1)} %get-tuple-element.20.xc, bf16[256,1024]{1,0:T(8,128)(2,1)} %get-tuple-element.21.z, ...), custom_call_target="tpu_custom_call" | custom-call | tf_op jit(solution)/shard_map/ssm0/pallas_call | solution.py:422
  61.6 55.6 %middle.1 = (bf16[256,1024]{1,0:T(8,128)(2,1)}, bf16[256,1024]{1,0:T(8,128)(2,1)}, bf16[256,1024]{1,0:T(8,128)(2,1)}, f32[2,288,128]{2,1,0:T(8,128)}, f32[32,4096]{1,0:T(8,128)}) custom-call(bf16[256,1024]{1,0:T(8,128)(2,1)} %get-tuple-element.22.yg, bf16[2,1024,4096]{2,1,0:T(8,128)(2,1)} %w_out.3, f32[256,4096]{1,0:T(8,128)} %resid.3, ...), custom_call_target="tpu_custom_call" | custom-call | tf_op jit(solution)/shard_map/middle/pallas_call | solution.py:403
  117.2 19.2 %ssm1.1 = (bf16[256,1024]{1,0:T(8,128)(2,1)}, bf16[2,3,256,1024]{3,2,1,0:T(8,128)(2,1)}, f32[2,256,16,1024]{3,2,1,0:T(8,128)}) custom-call(f32[2,288,128]{2,1,0:T(8,128)} %get-tuple-element.23.p, bf16[256,1024]{1,0:T(8,128)(2,1)} %get-tuple-element.24.x, bf16[256,1024]{1,0:T(8,128)(2,1)} %get-tuple-element.25.xc, ...), custom_call_target="tpu_custom_call", output_to_operand_aliasing={{1}: (10, {}), {2}: (11, {})} | custom-call | tf_op jit(solution)/shard_map/ssm1/pallas_call | solution.py:422
  136.5 32.8 %last.1 = bf16[256,4096]{1,0:T(8,128)(2,1)} custom-call(bf16[256,1024]{1,0:T(8,128)(2,1)} %get-tuple-element.29.yg, bf16[2,1024,4096]{2,1,0:T(8,128)(2,1)} %w_out.3, f32[32,4096]{1,0:T(8,128)} %get-tuple-element.30.oshard), custom_call_target="tpu_custom_call" | custom-call | tf_op jit(solution)/shard_map/last/pallas_call | solution.py:414
  169.3 5.6 %convert_add_fusion = f32[256,4096]{1,0:T(8,128)} fusion(f32[256,4096]{1,0:T(8,128)} %resid.3, bf16[256,4096]{1,0:T(8,128)(2,1)} %last.1), kind=kLoop, calls=%fused_computation | loop fusion | flops 2097152 | bytes 10485760 | tf_op jit(solution)/shard_map/add | solution.py:450

commit v2 on v1

v2 whole, which is shorter than its diff:
```python
import functools

import jax
import jax.numpy as jnp
from jax import lax
from jax.experimental import pallas as pl
from jax.experimental.pallas import tpu as pltpu
from jax.sharding import PartitionSpec as P

F32 = jnp.float32
BF16 = jnp.bfloat16
MESH = pl.DeviceIdType.MESH
VMEM = pl.BlockSpec(memory_space=pltpu.VMEM)
ANY = pl.BlockSpec(memory_space=pltpu.HBM)
DMA = pltpu.SemaphoreType.DMA

TOK = 256
DIM = 4096
CH = 1024
PW = 288
NST = 16
RANK = 256
NCH = 4
CW = DIM // NCH
NW = 8
KD = 256
NB = 16
TB = TOK // NB
AHEAD = (NB, 9)


def rows(start, size):
    return pl.ds(pl.multiple_of(start, size), size)


def place():
    me = lax.axis_index("tp")
    core = lax.rem(me, 2)
    xb = lax.rem(lax.div(me, 2), 2)
    yb = lax.div(me, 4)
    partner = me + 1 - 2 * core
    xn = me + 2 - 4 * xb
    yn = me + 4 - 8 * yb
    first = xn * (1 - core) + yn * core
    second = yn * (1 - core) + xn * core
    fb = xb * (1 - core) + yb * core
    sb = yb * (1 - core) + xb * core
    return core, fb, sb, partner, first, second


def enter(peers):
    barrier = pltpu.get_barrier_semaphore()
    for peer in peers:
        pl.semaphore_signal(barrier, inc=1, device_id={"tp": peer}, device_id_type=MESH)
    return lambda: pl.semaphore_wait(barrier, len(peers))


def remote(src, dst, sems, idx, to):
    return pltpu.make_async_remote_copy(
        src_ref=src, dst_ref=dst, send_sem=sems.at[0, idx], recv_sem=sems.at[1, idx],
        device_id={"tp": to}, device_id_type=MESH)


def spread(parity):
    src = lax.broadcasted_iota(jnp.int32, (128, 256), 0)
    dst = lax.broadcasted_iota(jnp.int32, (128, 256), 1)
    return jnp.where(dst == 2 * src + parity, 1.0, 0.0).astype(BF16)


def proj_steps(lo, hi, parity, acc, h, w):
    sel = spread(parity)

    def step(i, carry):
        cols = rows(i * KD, KD)
        hc = h[:, cols]
        lhs = jnp.concatenate(
            [jnp.dot(hc[:, j * 128:(j + 1) * 128], sel, preferred_element_type=F32).astype(BF16)
             for j in range(KD // 128)], axis=1)
        wc = w[cols, :, 0:CH].reshape(2 * KD, CH)
        acc[...] += jnp.dot(lhs, wc, preferred_element_type=F32)
        return carry

    lax.fori_loop(lo, hi, step, 0)


def copies(pairs, sem):
    return [pltpu.make_async_copy(src, dst, sem.at[i]) for i, (src, dst) in enumerate(pairs)]


def start(group):
    for c in group:
        c.start()


def wait(group):
    for c in group:
        c.wait()


def w_in_copies(layer, w_in, w, sem):
    size = DIM // NW
    return copies([(w_in.at[layer, pl.ds(i * size, size)], w.at[pl.ds(i * size, size), :, pl.ds(0, CH)])
                   for i in range(NW)], sem)


def state_copies(layer, st, dst, sem, lo=0, hi=None):
    hi = AHEAD[layer] if hi is None else hi
    return copies([(st.at[layer, pl.ds(i * TB, TB)], dst.at[pl.ds(i * TB, TB)]) for i in range(lo, hi)], sem)


def conv_stage(layer, acc, cs, cwb, cbb, cw, cb, x, xc):
    cw[...] = cwb[layer].astype(F32)
    cb[...] = cbb[layer:layer + 1, :].astype(F32)

    def block(i, carry):
        r = rows(i * 32, 32)
        xv = acc[r, :].astype(BF16)
        x[r, :] = xv
        pre = cs[0, r, :].astype(F32) * cw[0:1, :]
        pre += cs[1, r, :].astype(F32) * cw[1:2, :]
        pre += cs[2, r, :].astype(F32) * cw[2:3, :]
        pre += xv.astype(F32) * cw[3:4, :]
        pre += cb[...]
        xc[r, :] = (pre * jax.nn.sigmoid(pre)).astype(BF16)
        return carry

    lax.fori_loop(0, TOK // 32, block, 0)


def p_stage(where, z_part, xc, wx, p, ptx, prx, psem):
    core, _, _, partner, first, second = where

    def half(index):
        return lax.dot_general(wx[...], xc[rows(index * 128, 128), :], (((1,), (1,)), ((), ())),
                               preferred_element_type=F32)

    ptx[0] = half(1 - core).astype(BF16)
    hop = remote(ptx.at[0], prx.at[0], psem, 0, partner)
    hop.start()
    p[core] = half(core)
    z_part(0)
    hop.wait()
    for k, to in ((1, first), (2, second), (3, partner)):
        p[core] += prx[k - 1].astype(F32)
        ptx[k] = p[core].astype(BF16)
        hop = remote(ptx.at[k], prx.at[k], psem, k, to)
        hop.start()
        z_part(k)
        hop.wait()
    p[1 - core] = prx[3].astype(F32)


def in_tail(layer, where, acc, h, w, cs, conv, wx, x, xc, z, p, ptx, prx, psem):
    conv_stage(layer, acc, cs, *conv, x, xc)
    acc[...] = jnp.zeros_like(acc)
    n = DIM // KD
    cuts = (0, n // 8, n // 2, n - n // 8, n)

    def z_part(k):
        proj_steps(cuts[k], cuts[k + 1], 1, acc, h, w)

    p_stage(where, z_part, xc, wx, p, ptx, prx, psem)

    def block(i, carry):
        r = rows(i * 32, 32)
        z[r, :] = acc[r, :].astype(BF16)
        return carry

    lax.fori_loop(0, TOK // 32, block, 0)


def first_kernel(resid, nw_hbm, w_in, cw_hbm, cb_hbm, wx_hbm, cs_hbm, st_hbm, x, xc, z, p, cs, st,
                 h, w, acc, rbuf, wx, nwb, nw, cwb, cbb, cw, cb, ptx, prx, wsem, rsem, lsem, ssem, psem):
    where = place()
    core, fb, sb, partner, first, second = where
    await_peers = enter((partner, first, second))
    small = copies([(nw_hbm, nwb), (cw_hbm, cwb), (cb_hbm, cbb), (wx_hbm.at[0], wx), (cs_hbm.at[0], cs)], lsem)
    small[0].start()
    nr = 8
    start(copies([(resid.at[pl.ds(i * 32, 32)], rbuf.at[pl.ds(i * 32, 32)]) for i in range(nr)], rsem))
    wcopies = w_in_copies(0, w_in, w, wsem)
    start(wcopies)
    start(small[1:])
    acc[...] = jnp.zeros_like(acc)
    small[0].wait()
    nw[...] = nwb[0:1, :].astype(F32)

    def norm_block(i, carry):
        pltpu.make_async_copy(resid.at[rows(i * 32, 32)], rbuf.at[rows(i * 32, 32)], rsem.at[i]).wait()
        for b in range(2):
            r = pl.ds(pl.multiple_of(i * 32 + b * 16, 16), 16)
            v = rbuf[r, :]
            scale = lax.rsqrt(jnp.mean(v * v, axis=-1, keepdims=True) + 1e-5)
            h[r, :] = (v * scale * nw[...]).astype(BF16)
        return carry

    lax.fori_loop(0, nr, norm_block, 0)
    per = DIM // NW // KD
    for i in range(NW):
        wcopies[i].wait()
        proj_steps(i * per, (i + 1) * per, 0, acc, h, w)
    scopies = state_copies(0, st_hbm, st, ssem)
    start(scopies)
    wait(small[1:])
    await_peers()
    in_tail(0, where, acc, h, w, cs, (cwb, cbb, cw, cb), wx, x, xc, z, p, ptx, prx, psem)
    wait(scopies)


def w_out_copies(layer, w_out, wout, sem):
    return copies([(w_out.at[layer, :, pl.ds(c * CW, CW)], wout.at[:, pl.ds(c * CW, CW)]) for c in range(NCH)], sem)


def reduce_scatter(where, await_peers, yg, wout, wcopies, own, tx0, rx0, tx1, rx1, tx2, rx2, rsem):
    core, fb, sb, partner, first, second = where
    col = [pl.ds(c * CW, CW) for c in range(NCH)]
    hop0 = [remote(tx0.at[:, col[c]], rx0.at[:, col[c]], rsem, c, partner) for c in range(NCH)]
    hop1 = [remote(tx1.at[:, col[c]], rx1.at[:, col[c]], rsem, NCH + c, first) for c in range(NCH)]
    hop2 = [remote(tx2.at[:, col[c]], rx2.at[:, col[c]], rsem, 2 * NCH + c, second) for c in range(NCH)]

    def product(c):
        wcopies[c].wait()
        wc = wout[:, col[c]]
        tx0[:, col[c]] = jnp.dot(yg[rows((1 - core) * 128, 128), :], wc, preferred_element_type=F32).astype(BF16)
        if c == 0:
            await_peers()
        hop0[c].start()
        own[:, col[c]] = jnp.dot(yg[rows(core * 128, 128), :], wc, preferred_element_type=F32)

    def stage1(c):
        hop0[c].wait()
        give, keep = rows((1 - fb) * 64, 64), rows(fb * 64, 64)
        tx1[:, col[c]] = (own[give, col[c]] + rx0[give, col[c]].astype(F32)).astype(BF16)
        hop1[c].start()
        own[keep, col[c]] += rx0[keep, col[c]].astype(F32)

    def stage2(c):
        hop1[c].wait()
        give, keep = (1 - sb) * 32, sb * 32
        tx2[:, col[c]] = (own[rows(fb * 64 + give, 32), col[c]] + rx1[rows(give, 32), col[c]].astype(F32)).astype(BF16)
        hop2[c].start()
        own[rows(fb * 64 + keep, 32), col[c]] += rx1[rows(keep, 32), col[c]].astype(F32)

    product(0)
    product(1)
    stage1(0)
    product(2)
    stage1(1)
    product(3)
    stage1(2)
    stage1(3)
    for c in range(NCH):
        stage2(c)
    mine = rows(fb * 64 + sb * 32, 32)
    for c in range(NCH):
        hop2[c].wait()
        own[mine, col[c]] += rx2[:, col[c]].astype(F32)


def all_gather(where, h, gsem, consume):
    core, fb, sb, partner, first, second = where
    col = [pl.ds(c * CW, CW) for c in range(NCH)]
    base = core * 128

    def hops(k, begin, size, to):
        part = [h.at[rows(begin, size), col[c]] for c in range(NCH)]
        return [remote(part[c], part[c], gsem, k * NCH + c, to) for c in range(NCH)]

    hop0 = hops(0, base + fb * 64 + sb * 32, 32, second)
    hop1 = hops(1, base + fb * 64, 64, first)
    hop2 = hops(2, base, 128, partner)
    for c in range(NCH):
        hop0[c].start()
    for c in range(NCH):
        hop0[c].wait()
        hop1[c].start()
    for c in range(NCH):
        hop1[c].wait()
        hop2[c].start()
    for c in range(NCH):
        hop2[c].wait()
        consume(c)


def my_rows(where):
    core, fb, sb = where[:3]
    for b in range(2):
        off = fb * 64 + sb * 32 + b * 16
        yield pl.ds(pl.multiple_of(off, 16), 16), pl.ds(pl.multiple_of(core * 128 + off, 16), 16), pl.ds(b * 16, 16)


def middle_kernel(yg, w_out, resid, nw_hbm, w_in, cw_hbm, cb_hbm, wx_hbm, cs_hbm, st_hbm,
                  x, xc, z, p, cs, st, oshard,
                  wout, own, tx0, rx0, tx1, rx1, tx2, rx2, rmine,
                  h, w, acc, wx, nwb, nw, cwb, cbb, cw, cb, ptx, prx, osem, wsem, lsem, ssem, rsem, gsem, psem):
    where = place()
    core, fb, sb, partner, first, second = where
    await_peers = enter((partner, first, second))
    ocopies = w_out_copies(0, w_out, wout, osem)
    start(ocopies)
    row0 = core * 128 + fb * 64 + sb * 32
    small = copies([(nw_hbm, nwb), (cw_hbm, cwb), (cb_hbm, cbb), (wx_hbm.at[1], wx), (cs_hbm.at[1], cs),
                    (resid.at[rows(row0, 32)], rmine)], lsem)
    start(small)
    wcopies = w_in_copies(1, w_in, w, wsem)
    start(wcopies)
    reduce_scatter(where, await_peers, yg, wout, ocopies, own, tx0, rx0, tx1, rx1, tx2, rx2, rsem)
    wait(small)
    nw[...] = nwb[1:2, :].astype(F32)
    for sub, whole, part in my_rows(where):
        o = own[sub, :]
        oshard[part, :] = o
        v = o + rmine[part, :]
        scale = lax.rsqrt(jnp.mean(v * v, axis=-1, keepdims=True) + 1e-5)
        h[whole, :] = (v * scale * nw[...]).astype(BF16)
    wait(wcopies)
    scopies = state_copies(1, st_hbm, st, ssem)
    start(scopies)
    acc[...] = jnp.zeros_like(acc)
    per = CW // KD
    all_gather(where, h, gsem, lambda c: proj_steps(c * per, (c + 1) * per, 0, acc, h, w))
    in_tail(1, where, acc, h, w, cs, (cwb, cbb, cw, cb), wx, x, xc, z, p, ptx, prx, psem)
    wait(scopies)


def last_kernel(yg, oshard, w_out, resid, out, wout, own, tx0, rx0, tx1, rx1, tx2, rx2, total, rbuf, osem, lsem, rsem, gsem):
    where = place()
    core, fb, sb, partner, first, second = where
    await_peers = enter((partner, first, second))
    ocopies = w_out_copies(1, w_out, wout, osem)
    start(ocopies)
    rcopy = pltpu.make_async_copy(resid, rbuf, lsem.at[0])
    rcopy.start()
    reduce_scatter(where, await_peers, yg, wout, ocopies, own, tx0, rx0, tx1, rx1, tx2, rx2, rsem)
    for sub, whole, part in my_rows(where):
        total[whole, :] = (own[sub, :] + oshard[part, :]).astype(BF16)
    rcopy.wait()

    def consume(c):
        col = pl.ds(c * CW, CW)

        def block(i, carry):
            r = rows(i * 32, 32)
            out[r, col] = rbuf[r, col] + total[r, col].astype(F32)
            return carry

        lax.fori_loop(0, TOK // 32, block, 0)

    all_gather(where, total, gsem, consume)


def ssm_kernel(layer, x, xc, z, p, cs, st, wdt_hbm, bdt_hbm, alog_hbm, dskip_hbm, st_hbm, *refs):
    if layer:
        refs = refs[2:]
    yg, conv_out, st_out, new, dt_raw, dts, us, ys, a, bc, wdt, bdt, dskip, bdt1, dskip1, lsem, osem, csem, isem = refs
    small = copies([(bdt_hbm, bdt), (dskip_hbm, dskip), (alog_hbm.at[layer], a), (wdt_hbm.at[layer], wdt)], lsem)
    start(small)
    ahead = AHEAD[layer]
    start(state_copies(layer, st_hbm, new, isem, ahead, NB))
    couts = copies([(cs.at[pl.ds(1, 2)], conv_out.at[layer, pl.ds(0, 2)]), (x, conv_out.at[layer, 2])], csem)
    start(couts)
    for hf in range(2):
        for k in range(2):
            v = p[hf, RANK + k * NST:RANK + (k + 1) * NST, :]
            bc[hf, k * NST:(k + 1) * NST, :] = v * lax.rsqrt(jnp.mean(v * v, axis=0, keepdims=True) + 1e-6)
    wait(small)
    a[...] = -jnp.exp(a[...])
    bdt1[...] = bdt[layer:layer + 1, :]
    dskip1[...] = dskip[layer:layer + 1, :]
    for hf in range(2):
        low = p[hf, 0:RANK, :]
        low = low * lax.rsqrt(jnp.mean(low * low, axis=0, keepdims=True) + 1e-6)
        dt_raw[hf * 128:(hf + 1) * 128, :] = lax.dot_general(
            low.astype(BF16), wdt[...], (((0,), (0,)), ((), ())), preferred_element_type=F32)

    def out_copy(i):
        r = rows(i * TB, TB)
        return pltpu.make_async_copy(new.at[r], st_out.at[layer, r], osem.at[i])

    def block(src, i, carry):
        r = rows(i * TB, TB)
        if src is new:
            pltpu.make_async_copy(st_hbm.at[layer, r], new.at[r], isem.at[i - ahead]).wait()
        dt = jax.nn.softplus(dt_raw[r, :] + bdt1[...])
        xf = xc[r, :].astype(F32)
        dts[...] = dt
        us[...] = dt * xf
        hf = lax.div(i, NB // 2)
        shift = lax.rem(128 - lax.rem(i, NB // 2) * TB, 128)
        bct = pltpu.roll(bc[hf], shift, 1)
        for j in range(TB):
            bx = bct[0:NST, j:j + 1]
            cx = bct[NST:2 * NST, j:j + 1]
            s = jnp.exp(dts[j:j + 1, :] * a[...]) * src[i * TB + j] + us[j:j + 1, :] * bx
            new[i * TB + j] = s
            ys[j:j + 1, :] = jnp.sum(s * cx, axis=0, keepdims=True)
        out_copy(i).start()
        zf = z[r, :].astype(F32)
        y = ys[...] + dskip1[...] * xf
        yg[r, :] = (y * (zf * jax.nn.sigmoid(zf))).astype(BF16)
        return carry

    lax.fori_loop(0, ahead, functools.partial(block, st), 0)
    if ahead < NB:
        lax.fori_loop(ahead, NB, functools.partial(block, new), 0)
    wait(couts)
    for i in range(NB):
        out_copy(i).wait()


def sds(shape, dtype):
    return jax.ShapeDtypeStruct(shape, dtype)


def in_outs(layer):
    return (pltpu.VMEM((TOK, CH), BF16),) * 3 + (
        pltpu.VMEM((2, PW, 128), F32), pltpu.VMEM((3, TOK, CH), BF16), pltpu.VMEM((AHEAD[layer] * TB, NST, CH), F32))


PROJ_SCRATCH = [pltpu.VMEM((TOK, DIM), BF16), pltpu.VMEM((DIM, 2, CH + 128), BF16), pltpu.VMEM((TOK, CH), F32)]
P_SCRATCH = [pltpu.VMEM((PW, CH), BF16), pltpu.VMEM((2, DIM), BF16), pltpu.VMEM((1, DIM), F32),
             pltpu.VMEM((2, 4, CH), BF16), pltpu.VMEM((2, CH), BF16), pltpu.VMEM((4, CH), F32), pltpu.VMEM((1, CH), F32),
             pltpu.VMEM((4, PW, 128), BF16), pltpu.VMEM((4, PW, 128), BF16)]
RS_SCRATCH = [pltpu.VMEM((CH, DIM), BF16), pltpu.VMEM((128, DIM), F32)] + [pltpu.VMEM((n, DIM), BF16) for n in (128, 128, 64, 64, 32, 32)]


def params(mib, collective_id=None):
    if collective_id is None:
        return pltpu.CompilerParams(vmem_limit_bytes=mib << 20)
    return pltpu.CompilerParams(vmem_limit_bytes=mib << 20, collective_id=collective_id, has_side_effects=True)


def solution(mesh):
    def first_call(residual, *args):
        return pl.pallas_call(
            first_kernel, out_shape=in_outs(0), in_specs=[ANY] * 8, out_specs=(VMEM,) * 6,
            scratch_shapes=[*PROJ_SCRATCH, pltpu.VMEM((TOK, DIM), F32), *P_SCRATCH,
                            DMA((NW,)), DMA((8,)), DMA((5,)), DMA((NB,)), DMA((2, 4))],
            compiler_params=params(34, 0), name="first",
        )(residual, *args)

    def middle_call(yg, w_out, residual, *args):
        return pl.pallas_call(
            middle_kernel, out_shape=(*in_outs(1), pltpu.VMEM((32, DIM), F32)),
            in_specs=[VMEM] + [ANY] * 9, out_specs=(VMEM,) * 7,
            scratch_shapes=[*RS_SCRATCH, pltpu.VMEM((32, DIM), F32), *PROJ_SCRATCH, *P_SCRATCH,
                            DMA((NCH,)), DMA((NW,)), DMA((6,)), DMA((NB,)), DMA((2, 3 * NCH)), DMA((2, 3 * NCH)), DMA((2, 4))],
            compiler_params=params(47, 1), name="middle",
        )(yg, w_out, residual, *args)

    def last_call(yg, oshard, w_out, residual):
        return pl.pallas_call(
            last_kernel, out_shape=pltpu.VMEM((TOK, DIM), F32), in_specs=[VMEM, VMEM, ANY, ANY], out_specs=VMEM,
            scratch_shapes=[*RS_SCRATCH, pltpu.VMEM((TOK, DIM), BF16), pltpu.VMEM((TOK, DIM), F32),
                            DMA((NCH,)), DMA((1,)), DMA((2, 3 * NCH)), DMA((2, 3 * NCH))],
            compiler_params=params(56, 2), name="last",
        )(yg, oshard, w_out, residual)

    def ssm_call(layer, held, shapes, *args):
        return pl.pallas_call(
            functools.partial(ssm_kernel, layer),
            out_shape=(pltpu.VMEM((TOK, CH), BF16), *shapes),
            in_specs=[VMEM] * 6 + [ANY] * (5 + len(held)), out_specs=(VMEM, ANY, ANY),
            input_output_aliases={11: 1, 12: 2} if held else {},
            scratch_shapes=[pltpu.VMEM((TOK, NST, CH), F32), pltpu.VMEM((TOK, CH), F32), pltpu.VMEM((TB, CH), F32),
                            pltpu.VMEM((TB, CH), F32), pltpu.VMEM((TB, CH), F32), pltpu.VMEM((NST, CH), F32),
                            pltpu.VMEM((2, 2 * NST, 128), F32), pltpu.VMEM((RANK, CH), BF16),
                            pltpu.VMEM((2, CH), F32), pltpu.VMEM((2, CH), F32), pltpu.VMEM((1, CH), F32), pltpu.VMEM((1, CH), F32),
                            DMA((4,)), DMA((NB,)), DMA((2,)), DMA((NB,))],
            compiler_params=params(24), name=f"ssm{layer}",
        )(*args, *held)

    def device_step(residual, norm_w, w_in, conv_w, conv_b, w_x, w_dt, b_dt, a_log, d_skip, w_out, conv_state, ssm_state):
        cs = jnp.swapaxes(conv_state, 1, 2)
        wx = jnp.swapaxes(w_x, 1, 2)
        shapes = (sds(cs.shape, BF16), sds(ssm_state.shape, F32))
        in_args = (residual, norm_w, w_in, conv_w, conv_b, wx, cs, ssm_state)
        ssm_args = (w_dt, b_dt, a_log, d_skip, ssm_state)
        yg, *held = ssm_call(0, (), shapes, *first_call(*in_args), *ssm_args)
        *mid, oshard = middle_call(yg, w_out, *in_args)
        yg, conv_out, ssm_out = ssm_call(1, tuple(held), shapes, *mid, *ssm_args)
        return last_call(yg, oshard, w_out, residual), jnp.swapaxes(conv_out, 1, 2), ssm_out

    cache_spec = P(None, 'dp', None, 'tp')
    in_specs = (P('dp', None), P(None, None), P(None, None, None, 'tp'), P(None, None, 'tp'), P(None, 'tp'), P(None, 'tp', None), P(None, None, 'tp'), P(None, 'tp'), P(None, None, 'tp'), P(None, 'tp'), P(None, 'tp', None), cache_spec, cache_spec)
    out_specs = (P('dp', None), cache_spec, cache_spec)
    return jax.shard_map(device_step, mesh=mesh, in_specs=in_specs, out_specs=out_specs, check_vma=False)
```

time: 175 us -> 146 us (0.83)
  Pallas kernels: 159 us -> 139 us
  other arithmetic: 6.32 us -> 0 us
  local copies, waits for them, and re-layouts: 8.56 us -> 5.73 us
    pallas_call x5, Pallas kernels: 159 us -> 139 us  [the longest x1 54.4 us: middle_call(): pl.pallas_call(middle_kernel, out_shape=(*in_outs(1), pltpu.VMEM((32, DIM...]
    unnamed x0 -> x21, local copies, waits for them, and re-layouts: none -> 5.73 us
    add x1 -> x0, other arithmetic: 5.6 us -> none  [device_step(): return (residual + total.astype(F32), jnp.swapaxes(conv_out, 1, 2), ssm_out)]
    squeeze x3 -> x0, local copies, waits for them, and re-layouts: 4.38 us -> none  [the longest x1 2.24 us: ssm_args(): w_dt[layer]]
    slice x3 -> x0, local copies, waits for them, and re-layouts: 4.18 us -> none  [the longest x1 1.43 us: conv_args(): norm_w[layer:layer + 1]]
where the time goes in v2:
time: 146 us; the launch traced here: 145 us
  Pallas kernels  139 us (95%)
  local copies, waits for them, and re-layouts  5.73 us (4%)
    pallas_call x1, Pallas kernels, middle_call(): pl.pallas_call(middle_kernel, out_shape=(*in_outs(1), pltpu.VMEM((32, DIM...  54.4 us
    pallas_call x1, Pallas kernels, last_call(): pl.pallas_call(last_kernel, out_shape=pltpu.VMEM((TOK, DIM), F32), in_spe...  32.1 us
    pallas_call x1, Pallas kernels, first_call(): pl.pallas_call(first_kernel, out_shape=in_outs(0), in_specs=[ANY] * 8, ou...  29.8 us
    pallas_call x2, Pallas kernels, ssm_call(): pl.pallas_call(functools.partial(ssm_kernel, layer), out_shape=(pltpu.VME...  22.6 us
    unnamed x21, local copies, waits for them, and re-layouts  5.73 us

profile of v2, /device:TPU:0, one launch (start us, length us, event | category | flops | bytes accessed | tf_op | source)
XLA Modules:
  0.0 145.3 jit_solution(9384542233657313449)
XLA Ops:
  0.6 0.0 copy-start.5
  0.6 0.7 copy-done.5
  1.4 0.0 copy-start.6
  1.4 0.7 copy-done.6
  2.1 0.0 copy-start.9
  2.1 0.7 copy-done.9
  2.8 0.0 copy-start
  2.8 0.0 copy-start.2
  2.8 0.0 copy-start.7
  2.8 0.0 copy-start.8
  2.8 29.8 %first.1 = (bf16[256,1024]{1,0:T(8,128)(2,1)S(1)}, bf16[256,1024]{1,0:T(8,128)(2,1)S(1)}, bf16[256,1024]{1,0:T(8,128)(2,1)S(1)}, f32[2,288,128]{2,1,0:T(8,128)S(...) custom-call(f32[256,4096]{1,0:T(8,128)} %resid.5, bf16[2,4096]{1,0:T(2,128)(2,1)S(1)} %copy-done.5, ...), custom_call_target="tpu_custom_call" | custom-call | tf_op jit(solution)/shard_map/first/pallas_call | solution.py:435
  32.5 0.0 copy-done
  32.5 0.0 copy-done.2
  32.6 0.0 copy-done.7
  32.6 0.0 copy-done.8
  32.6 11.3 %ssm0.1 = (bf16[256,1024]{1,0:T(8,128)(2,1)S(1)}, bf16[2,3,256,1024]{3,2,1,0:T(8,128)(2,1)}, f32[2,256,16,1024]{3,2,1,0:T(8,128)}) custom-call(bf16[256,1024]{1,0:T(8,128)(2,1)S(1)} %get-tuple-element.22.x, bf16[256,1024]{1,0:T(8,128)(2,1)S(1)} %get-tuple-element.23.xc, bf16[256,1024]{1,0:T(8,128)(2,1)S(1)} %get-tuple-element.24.z, ...), custom_call_target="tpu_custom_call" | custom-call | tf_op jit(solution)/shard_map/ssm0/pallas_call | solution.py:460
  43.9 0.0 copy-start.1
  43.9 0.8 copy-done.1
  44.7 54.4 %middle.1 = (bf16[256,1024]{1,0:T(8,128)(2,1)S(1)}, bf16[256,1024]{1,0:T(8,128)(2,1)S(1)}, bf16[256,1024]{1,0:T(8,128)(2,1)S(1)}, f32[2,288,128]{2,1,0:T(8,128)S...) custom-call(bf16[256,1024]{1,0:T(8,128)(2,1)} %copy-done.1, ...), custom_call_target="tpu_custom_call" | custom-call | tf_op jit(solution)/shard_map/middle/pallas_call | solution.py:443
  99.1 0.0 copy-start.3
  99.1 11.3 %ssm1.1 = (bf16[256,1024]{1,0:T(8,128)(2,1)S(1)}, bf16[2,3,256,1024]{3,2,1,0:T(8,128)(2,1)}, f32[2,256,16,1024]{3,2,1,0:T(8,128)}) custom-call(bf16[256,1024]{1,0:T(8,128)(2,1)S(1)} %get-tuple-element.29.x, bf16[256,1024]{1,0:T(8,128)(2,1)S(1)} %get-tuple-element.30.xc, ...), custom_call_target="tpu_custom_call", output_to_operand_aliasing={{1}: (11, {}), {2}: (12, {})} | custom-call | tf_op jit(solution)/shard_map/ssm1/pallas_call | solution.py:460
  110.4 0.0 copy-done.3
  110.4 0.0 copy-start.4
  110.4 0.8 copy-done.4
  111.2 32.1 %last.1 = f32[256,4096]{1,0:T(8,128)S(1)} custom-call(bf16[256,1024]{1,0:T(8,128)(2,1)} %copy-done.4, f32[32,4096]{1,0:T(8,128)} %copy-done.3, bf16[2,1024,4096]{2,1,0:T(8,128)(2,1)} %w_out.3, f32[256,4096]{1,0:T(8,128)} %resid.5), custom_call_target="tpu_custom_call" | custom-call | tf_op jit(solution)/shard_map/last/pallas_call | solution.py:452
  143.3 2.0 %copy.21 = f32[256,4096]{1,0:T(8,128)} copy(f32[256,4096]{1,0:T(8,128)S(1)} %last.1) | data formatting | bytes 8388608
Async XLA Ops:
  0.6 0.7 copy-start.5
  1.4 0.7 copy-start.6
  2.1 0.7 copy-start.9
  2.8 29.8 %copy-start = (bf16[2,256,1024]{2,1,0:T(8,128)(2,1)S(1)}, bf16[2,256,1024]{2,1,0:T(8,128)(2,1)}, u32[]{:S(2)}) copy-start(bf16[2,256,1024]{2,1,0:T(8,128)(2,1)} %wdt_hbm.3) | copy-start | bytes 3145732
  2.8 29.8 %copy-start.2 = (f32[2,16,1024]{2,1,0:T(8,128)S(1)}, f32[2,16,1024]{2,1,0:T(8,128)}, u32[]{:S(2)}) copy-start(f32[2,16,1024]{2,1,0:T(8,128)} %alog_hbm.3) | copy-start | bytes 393220
  2.8 29.8 %copy-start.7 = (f32[2,1024]{1,0:T(2,128)S(1)}, f32[2,1024]{1,0:T(2,128)}, u32[]{:S(2)}) copy-start(f32[2,1024]{1,0:T(2,128)} %bdt_hbm.3) | copy-start | bytes 24580
  2.8 29.8 %copy-start.8 = (f32[2,1024]{1,0:T(2,128)S(1)}, f32[2,1024]{1,0:T(2,128)}, u32[]{:S(2)}) copy-start(f32[2,1024]{1,0:T(2,128)} %dskip_hbm.3) | copy-start | bytes 24580
  43.9 0.8 copy-start.1
  99.1 11.3 %copy-start.3 = (f32[32,4096]{1,0:T(8,128)}, f32[32,4096]{1,0:T(8,128)S(1)}, u32[]{:S(2)}) copy-start(f32[32,4096]{1,0:T(8,128)S(1)} %get-tuple-element.38.oshard) | copy-start | bytes 1572868
  110.4 0.8 copy-start.4

commit v3 on v2

--- a/solution.py
+++ b/solution.py
@@ -26,7 +26,7 @@
 KD = 256
 NB = 16
 TB = TOK // NB
-AHEAD = (NB, 9)
+AHEAD = (NB, 8)
 
 
 def rows(start, size):
@@ -76,7 +76,7 @@
         lhs = jnp.concatenate(
             [jnp.dot(hc[:, j * 128:(j + 1) * 128], sel, preferred_element_type=F32).astype(BF16)
              for j in range(KD // 128)], axis=1)
-        wc = w[cols, :, 0:CH].reshape(2 * KD, CH)
+        wc = w[rows(i * 2 * KD, 2 * KD), :]
         acc[...] += jnp.dot(lhs, wc, preferred_element_type=F32)
         return carry
 
@@ -97,10 +97,27 @@
         c.wait()
 
 
-def w_in_copies(layer, w_in, w, sem):
-    size = DIM // NW
-    return copies([(w_in.at[layer, pl.ds(i * size, size)], w.at[pl.ds(i * size, size), :, pl.ds(0, CH)])
-                   for i in range(NW)], sem)
+class WeightStream:
+    def __init__(self, layer, w_in, raw, w, sem):
+        self.raw, self.w, self.slots = raw, w, raw.shape[0]
+        self.size = DIM // NW
+        self.copy = [pltpu.make_async_copy(w_in.at[layer, pl.ds(i * self.size, self.size)], raw.at[i % self.slots], sem.at[i])
+                     for i in range(NW)]
+
+    def begin(self):
+        start(self.copy[:self.slots])
+
+    def lay_out(self, i):
+        self.copy[i].wait()
+        raw, w, slot, base = self.raw, self.w, i % self.slots, i * self.size
+
+        def block(k, carry):
+            w[rows(base * 2 + k * 256, 256), :] = raw[slot, rows(k * 128, 128)].reshape(256, CH)
+            return carry
+
+        lax.fori_loop(0, self.size // 128, block, 0)
+        if i + self.slots < NW:
+            self.copy[i + self.slots].start()
 
 
 def state_copies(layer, st, dst, sem, lo=0, hi=None):
@@ -170,7 +187,7 @@
 
 
 def first_kernel(resid, nw_hbm, w_in, cw_hbm, cb_hbm, wx_hbm, cs_hbm, st_hbm, x, xc, z, p, cs, st,
-                 h, w, acc, rbuf, wx, nwb, nw, cwb, cbb, cw, cb, ptx, prx, wsem, rsem, lsem, ssem, psem):
+                 h, raw, w, acc, rbuf, wx, nwb, nw, cwb, cbb, cw, cb, ptx, prx, wsem, rsem, lsem, ssem, psem):
     where = place()
     core, fb, sb, partner, first, second = where
     await_peers = enter((partner, first, second))
@@ -178,8 +195,8 @@
     small[0].start()
     nr = 8
     start(copies([(resid.at[pl.ds(i * 32, 32)], rbuf.at[pl.ds(i * 32, 32)]) for i in range(nr)], rsem))
-    wcopies = w_in_copies(0, w_in, w, wsem)
-    start(wcopies)
+    stream = WeightStream(0, w_in, raw, w, wsem)
+    stream.begin()
     start(small[1:])
     acc[...] = jnp.zeros_like(acc)
     small[0].wait()
@@ -197,7 +214,7 @@
     lax.fori_loop(0, nr, norm_block, 0)
     per = DIM // NW // KD
     for i in range(NW):
-        wcopies[i].wait()
+        stream.lay_out(i)
         proj_steps(i * per, (i + 1) * per, 0, acc, h, w)
     scopies = state_copies(0, st_hbm, st, ssem)
     start(scopies)
@@ -211,7 +228,7 @@
     return copies([(w_out.at[layer, :, pl.ds(c * CW, CW)], wout.at[:, pl.ds(c * CW, CW)]) for c in range(NCH)], sem)
 
 
-def reduce_scatter(where, await_peers, yg, wout, wcopies, own, tx0, rx0, tx1, rx1, tx2, rx2, rsem):
+def reduce_scatter(where, await_peers, yg, wout, wcopies, own, tx0, rx0, tx1, rx1, tx2, rx2, rsem, loads, fill):
     core, fb, sb, partner, first, second = where
     col = [pl.ds(c * CW, CW) for c in range(NCH)]
     hop0 = [remote(tx0.at[:, col[c]], rx0.at[:, col[c]], rsem, c, partner) for c in range(NCH)]
@@ -247,10 +264,16 @@
     product(2)
     stage1(1)
     product(3)
+    loads()
     stage1(2)
     stage1(3)
+    fill()
+    fill()
     for c in range(NCH):
         stage2(c)
+        fill()
+    fill()
+    fill()
     mine = rows(fb * 64 + sb * 32, 32)
     for c in range(NCH):
         hop2[c].wait()
@@ -292,7 +315,7 @@
 def middle_kernel(yg, w_out, resid, nw_hbm, w_in, cw_hbm, cb_hbm, wx_hbm, cs_hbm, st_hbm,
                   x, xc, z, p, cs, st, oshard,
                   wout, own, tx0, rx0, tx1, rx1, tx2, rx2, rmine,
-                  h, w, acc, wx, nwb, nw, cwb, cbb, cw, cb, ptx, prx, osem, wsem, lsem, ssem, rsem, gsem, psem):
+                  h, raw, w, acc, wx, nwb, nw, cwb, cbb, cw, cb, ptx, prx, osem, wsem, lsem, ssem, rsem, gsem, psem):
     where = place()
     core, fb, sb, partner, first, second = where
     await_peers = enter((partner, first, second))
@@ -302,9 +325,10 @@
     small = copies([(nw_hbm, nwb), (cw_hbm, cwb), (cb_hbm, cbb), (wx_hbm.at[1], wx), (cs_hbm.at[1], cs),
                     (resid.at[rows(row0, 32)], rmine)], lsem)
     start(small)
-    wcopies = w_in_copies(1, w_in, w, wsem)
-    start(wcopies)
-    reduce_scatter(where, await_peers, yg, wout, ocopies, own, tx0, rx0, tx1, rx1, tx2, rx2, rsem)
+    stream = WeightStream(1, w_in, raw, w, wsem)
+    pieces = iter(range(NW))
+    lay_out = lambda: stream.lay_out(next(pieces))
+    reduce_scatter(where, await_peers, yg, wout, ocopies, own, tx0, rx0, tx1, rx1, tx2, rx2, rsem, stream.begin, lay_out)
     wait(small)
     nw[...] = nwb[1:2, :].astype(F32)
     for sub, whole, part in my_rows(where):
@@ -313,7 +337,8 @@
         v = o + rmine[part, :]
         scale = lax.rsqrt(jnp.mean(v * v, axis=-1, keepdims=True) + 1e-5)
         h[whole, :] = (v * scale * nw[...]).astype(BF16)
-    wait(wcopies)
+    for i in pieces:
+        stream.lay_out(i)
     scopies = state_copies(1, st_hbm, st, ssem)
     start(scopies)
     acc[...] = jnp.zeros_like(acc)
@@ -330,8 +355,7 @@
     ocopies = w_out_copies(1, w_out, wout, osem)
     start(ocopies)
     rcopy = pltpu.make_async_copy(resid, rbuf, lsem.at[0])
-    rcopy.start()
-    reduce_scatter(where, await_peers, yg, wout, ocopies, own, tx0, rx0, tx1, rx1, tx2, rx2, rsem)
+    reduce_scatter(where, await_peers, yg, wout, ocopies, own, tx0, rx0, tx1, rx1, tx2, rx2, rsem, rcopy.start, lambda: None)
     for sub, whole, part in my_rows(where):
         total[whole, :] = (own[sub, :] + oshard[part, :]).astype(BF16)
     rcopy.wait()
@@ -352,7 +376,7 @@
 def ssm_kernel(layer, x, xc, z, p, cs, st, wdt_hbm, bdt_hbm, alog_hbm, dskip_hbm, st_hbm, *refs):
     if layer:
         refs = refs[2:]
-    yg, conv_out, st_out, new, dt_raw, dts, us, ys, a, bc, wdt, bdt, dskip, bdt1, dskip1, lsem, osem, csem, isem = refs
+    yg, conv_out, st_out, new, dts, us, ys, a, bc, wdt, bdt, dskip, bdt1, dskip1, lsem, osem, csem, isem = refs
     small = copies([(bdt_hbm, bdt), (dskip_hbm, dskip), (alog_hbm.at[layer], a), (wdt_hbm.at[layer], wdt)], lsem)
     start(small)
     ahead = AHEAD[layer]
@@ -370,8 +394,22 @@
     for hf in range(2):
         low = p[hf, 0:RANK, :]
         low = low * lax.rsqrt(jnp.mean(low * low, axis=0, keepdims=True) + 1e-6)
-        dt_raw[hf * 128:(hf + 1) * 128, :] = lax.dot_general(
-            low.astype(BF16), wdt[...], (((0,), (0,)), ((), ())), preferred_element_type=F32)
+        dts[hf * (NB // 2):(hf + 1) * (NB // 2)] = lax.dot_general(
+            low.astype(BF16), wdt[...], (((0,), (0,)), ((), ())), preferred_element_type=F32).reshape(NB // 2, TB, CH)
+
+    def dt_block(i, carry):
+        dt = jax.nn.softplus(dts[i] + bdt1[...])
+        dts[i] = dt
+        us[i] = dt * xc[rows(i * TB, TB), :].astype(F32)
+        return carry
+
+    lax.fori_loop(0, NB, dt_block, 0)
+    row = lax.broadcasted_iota(jnp.int32, (8, CH), 0)
+
+    def merge(level, one, two):
+        k = 1 << level
+        even = (row & k) == 0
+        return jnp.where(even, one, two) + pltpu.roll(jnp.where(even, two, one), 8 - k, 0)
 
     def out_copy(i):
         r = rows(i * TB, TB)
@@ -381,22 +419,26 @@
         r = rows(i * TB, TB)
         if src is new:
             pltpu.make_async_copy(st_hbm.at[layer, r], new.at[r], isem.at[i - ahead]).wait()
-        dt = jax.nn.softplus(dt_raw[r, :] + bdt1[...])
-        xf = xc[r, :].astype(F32)
-        dts[...] = dt
-        us[...] = dt * xf
         hf = lax.div(i, NB // 2)
         shift = lax.rem(128 - lax.rem(i, NB // 2) * TB, 128)
         bct = pltpu.roll(bc[hf], shift, 1)
-        for j in range(TB):
-            bx = bct[0:NST, j:j + 1]
-            cx = bct[NST:2 * NST, j:j + 1]
-            s = jnp.exp(dts[j:j + 1, :] * a[...]) * src[i * TB + j] + us[j:j + 1, :] * bx
-            new[i * TB + j] = s
-            ys[j:j + 1, :] = jnp.sum(s * cx, axis=0, keepdims=True)
+        for g in range(TB // 8):
+            stack = []
+            for j in range(g * 8, g * 8 + 8):
+                bx = bct[0:NST, j:j + 1]
+                cx = bct[NST:2 * NST, j:j + 1]
+                s = jnp.exp(dts[i, j:j + 1, :] * a[...]) * src[i * TB + j] + us[i, j:j + 1, :] * bx
+                new[i * TB + j] = s
+                sc = s * cx
+                level, v = 0, sc[0:8, :] + sc[8:16, :]
+                while stack and stack[-1][0] == level:
+                    v = merge(level, stack.pop()[1], v)
+                    level += 1
+                stack.append((level, v))
+            ys[g * 8:g * 8 + 8, :] = stack[0][1]
         out_copy(i).start()
         zf = z[r, :].astype(F32)
-        y = ys[...] + dskip1[...] * xf
+        y = ys[...] + dskip1[...] * xc[r, :].astype(F32)
         yg[r, :] = (y * (zf * jax.nn.sigmoid(zf))).astype(BF16)
         return carry
 
@@ -417,7 +459,11 @@
         pltpu.VMEM((2, PW, 128), F32), pltpu.VMEM((3, TOK, CH), BF16), pltpu.VMEM((AHEAD[layer] * TB, NST, CH), F32))
 
 
-PROJ_SCRATCH = [pltpu.VMEM((TOK, DIM), BF16), pltpu.VMEM((DIM, 2, CH + 128), BF16), pltpu.VMEM((TOK, CH), F32)]
+def proj_scratch(slots):
+    return [pltpu.VMEM((TOK, DIM), BF16), pltpu.VMEM((slots, DIM // NW, 2, CH), BF16), pltpu.VMEM((2 * DIM, CH), BF16),
+            pltpu.VMEM((TOK, CH), F32)]
+
+
 P_SCRATCH = [pltpu.VMEM((PW, CH), BF16), pltpu.VMEM((2, DIM), BF16), pltpu.VMEM((1, DIM), F32),
              pltpu.VMEM((2, 4, CH), BF16), pltpu.VMEM((2, CH), BF16), pltpu.VMEM((4, CH), F32), pltpu.VMEM((1, CH), F32),
              pltpu.VMEM((4, PW, 128), BF16), pltpu.VMEM((4, PW, 128), BF16)]
@@ -426,26 +472,26 @@
 
 def params(mib, collective_id=None):
     if collective_id is None:
-        return pltpu.CompilerParams(vmem_limit_bytes=mib << 20)
-    return pltpu.CompilerParams(vmem_limit_bytes=mib << 20, collective_id=collective_id, has_side_effects=True)
+        return pltpu.CompilerParams(vmem_limit_bytes=int(mib * 2 ** 20))
+    return pltpu.CompilerParams(vmem_limit_bytes=int(mib * 2 ** 20), collective_id=collective_id, has_side_effects=True)
 
 
 def solution(mesh):
     def first_call(residual, *args):
         return pl.pallas_call(
             first_kernel, out_shape=in_outs(0), in_specs=[ANY] * 8, out_specs=(VMEM,) * 6,
-            scratch_shapes=[*PROJ_SCRATCH, pltpu.VMEM((TOK, DIM), F32), *P_SCRATCH,
+            scratch_shapes=[*proj_scratch(4), pltpu.VMEM((TOK, DIM), F32), *P_SCRATCH,
                             DMA((NW,)), DMA((8,)), DMA((5,)), DMA((NB,)), DMA((2, 4))],
-            compiler_params=params(34, 0), name="first",
+            compiler_params=params(41.25, 0), name="first",
         )(residual, *args)
 
     def middle_call(yg, w_out, residual, *args):
         return pl.pallas_call(
             middle_kernel, out_shape=(*in_outs(1), pltpu.VMEM((32, DIM), F32)),
             in_specs=[VMEM] + [ANY] * 9, out_specs=(VMEM,) * 7,
-            scratch_shapes=[*RS_SCRATCH, pltpu.VMEM((32, DIM), F32), *PROJ_SCRATCH, *P_SCRATCH,
+            scratch_shapes=[*RS_SCRATCH, pltpu.VMEM((32, DIM), F32), *proj_scratch(2), *P_SCRATCH,
                             DMA((NCH,)), DMA((NW,)), DMA((6,)), DMA((NB,)), DMA((2, 3 * NCH)), DMA((2, 3 * NCH)), DMA((2, 4))],
-            compiler_params=params(47, 1), name="middle",
+            compiler_params=params(46, 1), name="middle",
         )(yg, w_out, residual, *args)
 
     def last_call(yg, oshard, w_out, residual):
@@ -453,7 +499,7 @@
             last_kernel, out_shape=pltpu.VMEM((TOK, DIM), F32), in_specs=[VMEM, VMEM, ANY, ANY], out_specs=VMEM,
             scratch_shapes=[*RS_SCRATCH, pltpu.VMEM((TOK, DIM), BF16), pltpu.VMEM((TOK, DIM), F32),
                             DMA((NCH,)), DMA((1,)), DMA((2, 3 * NCH)), DMA((2, 3 * NCH))],
-            compiler_params=params(56, 2), name="last",
+            compiler_params=params(52, 2), name="last",
         )(yg, oshard, w_out, residual)
 
     def ssm_call(layer, held, shapes, *args):
@@ -462,12 +508,12 @@
             out_shape=(pltpu.VMEM((TOK, CH), BF16), *shapes),
             in_specs=[VMEM] * 6 + [ANY] * (5 + len(held)), out_specs=(VMEM, ANY, ANY),
             input_output_aliases={11: 1, 12: 2} if held else {},
-            scratch_shapes=[pltpu.VMEM((TOK, NST, CH), F32), pltpu.VMEM((TOK, CH), F32), pltpu.VMEM((TB, CH), F32),
-                            pltpu.VMEM((TB, CH), F32), pltpu.VMEM((TB, CH), F32), pltpu.VMEM((NST, CH), F32),
+            scratch_shapes=[pltpu.VMEM((TOK, NST, CH), F32), pltpu.VMEM((NB, TB, CH), F32),
+                            pltpu.VMEM((NB, TB, CH), F32), pltpu.VMEM((TB, CH), F32), pltpu.VMEM((NST, CH), F32),
                             pltpu.VMEM((2, 2 * NST, 128), F32), pltpu.VMEM((RANK, CH), BF16),
                             pltpu.VMEM((2, CH), F32), pltpu.VMEM((2, CH), F32), pltpu.VMEM((1, CH), F32), pltpu.VMEM((1, CH), F32),
                             DMA((4,)), DMA((NB,)), DMA((2,)), DMA((NB,))],
-            compiler_params=params(24), name=f"ssm{layer}",
+            compiler_params=params(22), name=f"ssm{layer}",
         )(*args, *held)
 
     def device_step(residual, norm_w, w_in, conv_w, conv_b, w_x, w_dt, b_dt, a_log, d_skip, w_out, conv_state, ssm_state):

time: 146 us -> 138 us (0.945)
  Pallas kernels: 139 us -> 134 us
  local copies, waits for them, and re-layouts: 5.73 us -> 3.61 us
    pallas_call x1, Pallas kernels: 54.4 us -> 51.1 us  [middle_call(): pl.pallas_call(middle_kernel, out_shape=(*in_outs(1), pltpu.VMEM((32, DIM...]
    unnamed x21 -> x15, local copies, waits for them, and re-layouts: 5.73 us -> 3.61 us
    pallas_call x2, Pallas kernels: 22.6 us -> 21.1 us  [ssm_call(): pl.pallas_call(functools.partial(ssm_kernel, layer), out_shape=(pltpu.VME...]
where the time goes in v3:
time: 138 us
  Pallas kernels  134 us (97%)
  local copies, waits for them, and re-layouts  3.61 us (3%)
    pallas_call x1, Pallas kernels, middle_call(): pl.pallas_call(middle_kernel, out_shape=(*in_outs(1), pltpu.VMEM((32, DIM...  51.1 us
    pallas_call x1, Pallas kernels, last_call(): pl.pallas_call(last_kernel, out_shape=pltpu.VMEM((TOK, DIM), F32), in_spe...  32.1 us
    pallas_call x1, Pallas kernels, first_call(): pl.pallas_call(first_kernel, out_shape=in_outs(0), in_specs=[ANY] * 8, ou...  29.4 us
    pallas_call x2, Pallas kernels, ssm_call(): pl.pallas_call(functools.partial(ssm_kernel, layer), out_shape=(pltpu.VME...  21.1 us
    unnamed x15, local copies, waits for them, and re-layouts  3.61 us

profile of v3, /device:TPU:0, one launch (start us, length us, event | category | flops | bytes accessed | tf_op | source)
XLA Modules:
  0.0 138.1 jit_solution(16141086939432837338)
XLA Ops:
  0.6 0.0 copy-start
  0.6 0.0 copy-start.2
  0.7 0.0 copy-start.5
  0.7 0.0 copy-start.6
  0.7 29.4 %first.1 = (bf16[256,1024]{1,0:T(8,128)(2,1)S(1)}, bf16[256,1024]{1,0:T(8,128)(2,1)S(1)}, bf16[256,1024]{1,0:T(8,128)(2,1)S(1)}, f32[2,288,128]{2,1,0:T(8,128)S(...) custom-call(f32[256,4096]{1,0:T(8,128)} %resid.5, bf16[2,4096]{1,0:T(2,128)(2,1)} %nw_hbm.3, ...), custom_call_target="tpu_custom_call" | custom-call | tf_op jit(solution)/shard_map/first/pallas_call | solution.py:481
  30.1 0.0 copy-done
  30.1 0.0 copy-done.2
  30.1 0.0 copy-done.5
  30.1 0.0 copy-done.6
  30.1 10.6 %ssm0.1 = (bf16[256,1024]{1,0:T(8,128)(2,1)S(1)}, bf16[2,3,256,1024]{3,2,1,0:T(8,128)(2,1)}, f32[2,256,16,1024]{3,2,1,0:T(8,128)}) custom-call(bf16[256,1024]{1,0:T(8,128)(2,1)S(1)} %get-tuple-element.22.x, bf16[256,1024]{1,0:T(8,128)(2,1)S(1)} %get-tuple-element.23.xc, bf16[256,1024]{1,0:T(8,128)(2,1)S(1)} %get-tuple-element.24.z, ...), custom_call_target="tpu_custom_call" | custom-call | tf_op jit(solution)/shard_map/ssm0/pallas_call | solution.py:506
  40.7 0.0 copy-start.1
  40.7 0.8 copy-done.1
  41.5 51.1 %middle.1 = (bf16[256,1024]{1,0:T(8,128)(2,1)S(1)}, bf16[256,1024]{1,0:T(8,128)(2,1)S(1)}, bf16[256,1024]{1,0:T(8,128)(2,1)S(1)}, f32[2,288,128]{2,1,0:T(8,128)S...) custom-call(bf16[256,1024]{1,0:T(8,128)(2,1)} %copy-done.1, ...), custom_call_target="tpu_custom_call" | custom-call | tf_op jit(solution)/shard_map/middle/pallas_call | solution.py:489
  92.6 0.0 copy-start.3
  92.6 10.5 %ssm1.1 = (bf16[256,1024]{1,0:T(8,128)(2,1)S(1)}, bf16[2,3,256,1024]{3,2,1,0:T(8,128)(2,1)}, f32[2,256,16,1024]{3,2,1,0:T(8,128)}) custom-call(bf16[256,1024]{1,0:T(8,128)(2,1)S(1)} %get-tuple-element.29.x, bf16[256,1024]{1,0:T(8,128)(2,1)S(1)} %get-tuple-element.30.xc, ...), custom_call_target="tpu_custom_call", output_to_operand_aliasing={{1}: (11, {}), {2}: (12, {})} | custom-call | tf_op jit(solution)/shard_map/ssm1/pallas_call | solution.py:506
  103.2 0.0 copy-done.3
  103.2 0.0 copy-start.4
  103.2 0.8 copy-done.4
  104.0 32.1 %last.1 = f32[256,4096]{1,0:T(8,128)S(1)} custom-call(bf16[256,1024]{1,0:T(8,128)(2,1)} %copy-done.4, f32[32,4096]{1,0:T(8,128)} %copy-done.3, bf16[2,1024,4096]{2,1,0:T(8,128)(2,1)} %w_out.3, f32[256,4096]{1,0:T(8,128)} %resid.5), custom_call_target="tpu_custom_call" | custom-call | tf_op jit(solution)/shard_map/last/pallas_call | solution.py:498
  136.1 2.0 %copy.21 = f32[256,4096]{1,0:T(8,128)} copy(f32[256,4096]{1,0:T(8,128)S(1)} %last.1) | data formatting | bytes 8388608
Async XLA Ops:
  0.6 29.4 %copy-start = (bf16[2,256,1024]{2,1,0:T(8,128)(2,1)S(1)}, bf16[2,256,1024]{2,1,0:T(8,128)(2,1)}, u32[]{:S(2)}) copy-start(bf16[2,256,1024]{2,1,0:T(8,128)(2,1)} %wdt_hbm.3) | copy-start | bytes 3145732
  0.6 29.4 %copy-start.2 = (f32[2,16,1024]{2,1,0:T(8,128)S(1)}, f32[2,16,1024]{2,1,0:T(8,128)}, u32[]{:S(2)}) copy-start(f32[2,16,1024]{2,1,0:T(8,128)} %alog_hbm.3) | copy-start | bytes 393220
  0.7 29.4 %copy-start.5 = (f32[2,1024]{1,0:T(2,128)S(1)}, f32[2,1024]{1,0:T(2,128)}, u32[]{:S(2)}) copy-start(f32[2,1024]{1,0:T(2,128)} %bdt_hbm.3) | copy-start | bytes 24580
  0.7 29.4 %copy-start.6 = (f32[2,1024]{1,0:T(2,128)S(1)}, f32[2,1024]{1,0:T(2,128)}, u32[]{:S(2)}) copy-start(f32[2,1024]{1,0:T(2,128)} %dskip_hbm.3) | copy-start | bytes 24580
  40.7 0.8 copy-start.1
  92.6 10.5 %copy-start.3 = (f32[32,4096]{1,0:T(8,128)}, f32[32,4096]{1,0:T(8,128)S(1)}, u32[]{:S(2)}) copy-start(f32[32,4096]{1,0:T(8,128)S(1)} %get-tuple-element.38.oshard) | copy-start | bytes 1572868
  103.2 0.8 copy-start.4
